TPU v7x, 32 devices: a whole 2x2x4 slice. The times are simulated.
32 devices in a mesh: dp: 16 (over z, x, core), section: 2 (over y).
Axes of the slice: x: 2, y: 2, z: 4, core: 2. Of those that a mesh axis runs over, the one named last changes fastest.
Arguments:
- samples: bfloat16 [128, 512], P('dp'), may hold values from -6 to 6
- targets: bfloat16 [128, 512], P('dp'), may hold values from -6 to 6
- jacobian_targets: bfloat16 [128, 128, 512], P('dp'), may hold values from -0.1796875 to 0.1796875
- directions: int32 [128, 128], P('dp'), may hold values from 0 to 511
- plan: int32 [16, 8], P('dp'), may hold values from 0 to 7, each once within a row
- weights: bfloat16 [2, 512, 8192], P('section'), may hold values from -1 to 1
Outputs:
- gradients: float32 [2, 512, 8192], P('section', 'dp')
Inputs may be any that keep to these rules, and one draw needn't show every extreme that they name: `plan`: each row is a permutation of 0 to 7.
All inputs are finite; a program needn't handle non-finite values.
Results may differ from a plain program's by a relative error of at most 0.0034.
Values may be sent and summed in bfloat16 or wider, within the bound.
A program may use at most 128 MiB of HBM per device.

v0:
```python
import functools

import jax
import jax.numpy as jnp
from jax import lax
from jax.experimental import pallas as pl
from jax.experimental.pallas import tpu as pltpu
from jax.sharding import PartitionSpec as P

MICRO = 4
GROUP = 4
PAD = 16
PIECES = 4

jacobian_weight = 32.0

VMEM = pl.BlockSpec(memory_space=pltpu.VMEM)
ANY = pl.BlockSpec(memory_space=pl.ANY)


def place():
    dp, sec = lax.axis_index("dp"), lax.axis_index("section")
    g = lax.rem(dp, GROUP)
    return dp, sec, g, dp - g


def greet(peers):
    barrier = pltpu.get_barrier_semaphore()
    for dp, sec in peers:
        pl.semaphore_signal(barrier, inc=1, device_id={"dp": dp, "section": sec})
    pl.semaphore_wait(barrier, len(peers))


def remote(src, dst, send, recv, dp, sec):
    return pltpu.make_async_remote_copy(
        src_ref=src, dst_ref=dst, send_sem=send, recv_sem=recv,
        device_id={"dp": dp, "section": sec},
    )


def spread_kernel(
    n_sec, n_s, plan, samples, directions, weight, packs, both,
    psend, precv, wsend, wrecv, zsend, zrecv, local,
):
    dp, sec, g, base = place()
    _, reduced, cols = both.shape
    parity = lax.rem(dp // GROUP, 2)
    twin = (dp + GROUP * (1 - 2 * parity), sec)
    near = [(base + lax.rem(g + k, GROUP), sec) for k in range(1, GROUP)]
    far = [(dp, lax.rem(sec + k, n_sec)) for k in range(1, n_sec)]
    greet(near + far + [twin])
    piece = reduced // 2 // PIECES

    def part(section):
        start = pl.multiple_of((section * GROUP + g) * cols, cols)
        return weight.at[0, :, pl.ds(start, cols)]

    def rows_of(c):
        return pl.ds(pl.multiple_of(parity * (reduced // 2) + c * piece, piece), piece)

    sent = []
    for c in range(PIECES):
        for k, (d, s) in enumerate(far):
            i = k * PIECES + c
            sent.append(
                remote(
                    part(s).at[rows_of(c)], both.at[sec, rows_of(c)],
                    wsend.at[i], wrecv.at[i], d, s,
                )
            )
    for copy in sent:
        copy.start()
    own = pltpu.make_async_copy(part(sec), both.at[sec], local)
    own.start()
    every = jnp.concatenate(
        [samples[...].astype(jnp.float32), directions[...].astype(jnp.float32)], axis=1
    )
    row = lax.broadcasted_iota(jnp.int32, every.shape, 0)
    packed = jnp.zeros_like(every)
    for k in range(MICRO):
        line = jnp.sum(jnp.where(row == plan[0, k], every, 0.0), axis=0, keepdims=True)
        packed = jnp.where(row == k, line, packed)
    packs[g] = packed
    own.wait()
    shared = [
        remote(packs.at[g], packs.at[g], psend.at[k], precv.at[k], d, s)
        for k, (d, s) in enumerate(near)
    ]
    for copy in shared:
        copy.start()
    passed = []
    for c in range(PIECES):
        for k in range(n_sec - 1):
            i = k * PIECES + c
            sent[c * (n_sec - 1) + k].wait_recv()
            came = both.at[lax.rem(sec + n_sec - 1 - k, n_sec), rows_of(c)]
            copy = remote(came, came, zsend.at[i], zrecv.at[i], *twin)
            copy.start()
            passed.append(copy)
    for copy in shared + passed:
        copy.wait()
    for copy in sent:
        copy.wait_send()


def onehot_columns(directions_row, reduced):
    rows = lax.broadcasted_iota(jnp.int32, (reduced, directions_row.shape[1]), 0)
    return (rows == directions_row.astype(jnp.int32)).astype(jnp.float32).astype(jnp.bfloat16)


def stack_rows(lines, shape):
    row = lax.broadcasted_iota(jnp.int32, shape, 0)
    result = jnp.zeros(shape, jnp.float32)
    for i, line in enumerate(lines):
        result = jnp.where(row == i, line, result)
    return result


def pack_row(packs, block, spt, i):
    return packs[lax.rem(block, GROUP), pl.ds(block // GROUP * spt + i, 1), :]


def forward_kernel(
    spt, plan, sec, packs, both, jac_target, targets,
    act, picked_out, slopes, partial, jac_out, target_out,
):
    block = pl.program_id(0)
    tangents, reduced = jac_target.shape[1:]
    rows = spt * tangents
    jac_out[...] = jac_target[...]

    @pl.when(block == 0)
    def _():
        all_targets = targets[...].astype(jnp.float32)
        row = lax.broadcasted_iota(jnp.int32, all_targets.shape, 0)
        lines = [
            jnp.sum(
                jnp.where(row == plan[0, sec[0] * spt + i], all_targets, 0.0),
                axis=0, keepdims=True,
            )
            for i in range(spt)
        ]
        target_out[...] = stack_rows(lines, target_out.shape).astype(jnp.bfloat16)

    packed = [pack_row(packs, block, spt, i) for i in range(spt)]
    xs = stack_rows([p[:, :reduced] for p in packed], (PAD, reduced)).astype(jnp.bfloat16)
    linear = jnp.dot(xs, both[0], preferred_element_type=jnp.float32)
    squash = jax.nn.sigmoid(linear)
    first = squash * (1.0 + linear * (1.0 - squash))
    second = squash * (1.0 - squash) * (2.0 + linear * (1.0 - 2.0 * squash))
    slopes[0, 0:PAD] = first
    slopes[0, PAD : 2 * PAD] = second
    for i in range(spt):
        lo = i * tangents
        picked = lax.dot_general(
            onehot_columns(packed[i][:, reduced:], reduced), both[0],
            (((0,), (0,)), ((), ())), preferred_element_type=jnp.float32,
        )
        picked_out[0, lo : lo + tangents] = picked.astype(jnp.bfloat16)
        act[0, lo : lo + tangents] = (first[i : i + 1] * picked).astype(jnp.bfloat16)
    act[0, rows:] = (linear * squash).astype(jnp.bfloat16)
    partial[0] = lax.dot_general(
        act[0], both[1], (((1,), (1,)), ((), ())), preferred_element_type=jnp.float32
    ).astype(jnp.bfloat16)


def step_kernel(
    n_sec, n_s, spt,
    partial, jac_target, target, packs, both, act_hbm, picked_hbm, slopes_hbm, out,
    first_in, sums, second_in, misfit, act, picked, slopes, total, grads,
    tails, xs_all, inbox, halves, finished,
    s1, r1, s2, r2, s3, r3, s4, r4, s5, r5, s6, r6, load, local,
):
    dp, sec, g, base = place()
    s = dp // GROUP
    half = GROUP // 2
    team = n_sec * GROUP
    quads = n_sec * half
    core = lax.rem(g, 2)
    q = sec * half + g // 2
    partner = (base + (g // 2) * 2 + (1 - core), sec)
    rows, reduced = spt * jac_target.shape[1], both.shape[1]
    tangents = rows // spt
    cols = both.shape[2]
    slab = reduced // n_s
    own_rows = slab // GROUP
    f32, bf16 = jnp.float32, jnp.bfloat16
    over_rows = (((0,), (0,)), ((), ()))

    def quad(k):
        other = lax.rem(q + k, quads)
        return other // half, lax.rem(other, half)

    def device(k):
        l, h = quad(k)
        return base + h * 2 + core, l

    def block(k, c):
        l, h = quad(k)
        return l * GROUP + h * 2 + c

    if n_s == 4:
        mate = s + 1 - 2 * lax.rem(s, 2)
        opposite = lax.rem(s + 2, 4)
        mate_opposite = lax.rem(mate + 2, 4)
        others = [mate, opposite]
    else:
        others = [lax.rem(s + k, n_s) for k in range(1, n_s)]
    team_peers = [
        ((base + lax.rem(g + k, GROUP)), lax.rem(sec + j, n_sec))
        for j in range(n_sec) for k in range(GROUP) if j or k
    ]
    greet(team_peers + [(o * GROUP + g, sec) for o in others])
    loads = [
        pltpu.make_async_copy(a, b, load.at[i])
        for i, (a, b) in enumerate(((act_hbm, act), (picked_hbm, picked), (slopes_hbm, slopes)))
    ]

    across = [
        remote(partial.at[block(k, 1 - core)], first_in.at[k], s1.at[k], r1.at[k], *partner)
        for k in range(quads)
    ]
    for k in list(range(1, quads)) + [0]:
        across[k].start()
    for copy in loads:
        copy.start()
    away = [None] + [
        remote(sums.at[k - 1], second_in.at[k - 1], s2.at[k - 1], r2.at[k - 1], *device(k))
        for k in range(1, quads)
    ]
    for k in range(1, quads):
        across[k].wait_recv()
        sums[k - 1] = (
            partial[block(k, core)].astype(f32) + first_in[k].astype(f32)
        ).astype(bf16)
        away[k].start()
    across[0].wait_recv()
    for k in range(quads):
        across[k].wait_send()
    mine = block(0, core)
    for k in range(1, quads):
        away[k].wait_recv()

    def whole(lo, hi):
        value = partial[mine, lo:hi].astype(f32) + first_in[0, lo:hi].astype(f32)
        for k in range(1, quads):
            value = value + second_in[k - 1, lo:hi].astype(f32)
        return value

    for i in range(spt):
        lo, hi = i * tangents, (i + 1) * tangents
        misfit[mine, lo:hi] = (
            jacobian_weight * (whole(lo, hi) - jac_target[i].astype(f32))
        ).astype(bf16)
    misfit[mine, rows:] = (whole(rows, rows + PAD) - target[...].astype(f32)).astype(bf16)
    for k in range(1, quads):
        away[k].wait_send()
    gather = [
        remote(misfit.at[mine], misfit.at[mine], s3.at[k - 1], r3.at[k - 1], *device(k))
        for k in range(1, quads)
    ]
    for copy in gather:
        copy.start()
    passed = [remote(misfit.at[mine], misfit.at[mine], s4.at[0], r4.at[0], *partner)]
    passed[0].start()
    for copy in loads:
        copy.wait()

    def last_of(b):
        total[1] += lax.dot_general(misfit[b], act[b], over_rows, preferred_element_type=f32)

    total[...] = jnp.zeros_like(total)
    last_of(mine)
    passed[0].wait_recv()
    last_of(block(0, 1 - core))
    for k in range(1, quads):
        gather[k - 1].wait_recv()
        came = block(quads - k, core)
        copy = remote(misfit.at[came], misfit.at[came], s4.at[k], r4.at[k], *partner)
        copy.start()
        passed.append(copy)
        last_of(came)
    for k in range(1, quads):
        passed[k].wait_recv()
        last_of(block(quads - k, 1 - core))

    def slab_of(owner):
        return pl.ds(pl.multiple_of(owner * slab, slab), slab)

    def link(layer, kind, source, to):
        i = layer * inbox.shape[1] + kind
        return remote(source, inbox.at[layer, kind], s5.at[i], r5.at[i], to * GROUP + g, sec)

    flights = {}

    def send_layer(layer):
        grads[layer] = total[layer].astype(bf16)
        if n_s == 4:
            flights[layer] = [
                link(layer, 0, grads.at[layer, slab_of(mate_opposite)], mate),
                link(layer, 1, grads.at[layer, slab_of(mate)], mate),
            ]
        else:
            flights[layer] = [
                link(layer, k, grads.at[layer, slab_of(o)], o) for k, o in enumerate(others)
            ]
        for copy in flights[layer]:
            copy.start()

    def relay(layer):
        if n_s == 4:
            flights[layer][0].wait_recv()
            halves[layer] = (
                grads[layer, slab_of(opposite), :].astype(f32) + inbox[layer, 0].astype(f32)
            ).astype(bf16)
            copy = link(layer, 2, halves.at[layer], opposite)
            copy.start()
            flights[layer].append(copy)

    columns = out.at[:, pl.ds(pl.multiple_of((sec * GROUP + g) * cols, cols), cols)]

    def hand(layer, k):
        h = lax.rem(g + k, GROUP)
        return remote(
            finished.at[layer * GROUP + h], columns,
            s6.at[layer * GROUP + k], r6.at[sec * GROUP + k], base + h, layer,
        )

    def keep():
        return pltpu.make_async_copy(finished.at[sec * GROUP + g], columns, local)

    def finish(layer):
        kinds = range(1, 3) if n_s == 4 else range(n_s - 1)
        for k in kinds:
            flights[layer][k].wait_recv()
        for h in range(GROUP):
            start = pl.multiple_of(s * slab + h * own_rows, own_rows)
            value = grads[layer, pl.ds(start, own_rows), :].astype(f32)
            for k in kinds:
                value = value + inbox[layer, k, h * own_rows : (h + 1) * own_rows].astype(f32)
            finished[layer * GROUP + h] = value
        for copy in flights[layer]:
            copy.wait_send()
        for k in range(1, GROUP):
            hand(layer, k).start()

        @pl.when(sec != layer)
        def _():
            hand(layer, 0).start()

        @pl.when(sec == layer)
        def _():
            keep().start()

    def pull(b, carry):
        cotangent = jnp.dot(misfit[b], both[1], preferred_element_type=f32)
        first = slopes[b, 0:PAD]
        second = slopes[b, PAD : 2 * PAD]
        lines = []
        chosen = []
        pulled = []
        packed = [pack_row(packs, b, spt, i) for i in range(spt)]
        for i in range(spt):
            lo = i * tangents
            part = cotangent[lo : lo + tangents]
            lines.append(
                jnp.sum(part * picked[b, lo : lo + tangents].astype(f32), axis=0, keepdims=True)
            )
            pulled.append((part * first[i : i + 1]).astype(bf16))
            chosen.append(onehot_columns(packed[i][:, reduced:], reduced))
        here = pl.ds(pl.multiple_of(b * PAD, PAD), PAD)
        tails[here, :] = (
            cotangent[rows:] * first + second * stack_rows(lines, first.shape)
        ).astype(bf16)
        xs_all[here, :] = stack_rows([p[:, :reduced] for p in packed], (PAD, reduced)).astype(bf16)
        total[0] += jnp.dot(
            jnp.concatenate(chosen, axis=1), jnp.concatenate(pulled, axis=0),
            preferred_element_type=f32,
        )
        return carry

    send_layer(1)
    lax.fori_loop(0, team // 2, pull, 0)
    relay(1)
    lax.fori_loop(team // 2, team, pull, 0)
    total[0] += lax.dot_general(
        xs_all[...], tails[...], over_rows, preferred_element_type=f32
    )
    send_layer(0)
    finish(1)
    relay(0)
    finish(0)

    for layer in range(n_sec):
        for k in range(1, GROUP):
            hand(layer, k).wait_send()

        @pl.when(sec != layer)
        def _():
            hand(layer, 0).wait_send()

    keep().wait()
    for j in range(n_sec):
        for k in range(GROUP):
            arrival = remote(
                finished.at[0], columns, s6.at[0], r6.at[j * GROUP + k], *partner
            )
            if k:
                arrival.wait_recv()
            else:

                @pl.when(sec != j)
                def _():
                    arrival.wait_recv()

    for copy in gather + passed:
        copy.wait_send()


def shards(n_dp, n_sec, samples, targets, jacobian_targets, directions, plan, weights):
    sec = lax.axis_index("section")
    _, reduced, width = weights.shape
    pool, tangents = directions.shape
    team = n_sec * GROUP
    cols = width // team
    n_s = n_dp // GROUP
    spt = MICRO // n_sec
    rows = spt * tangents
    high = rows + PAD
    dma = lambda n: pltpu.SemaphoreType.DMA((n,))
    f32, bf16 = jnp.float32, jnp.bfloat16
    shape = jax.ShapeDtypeStruct
    limit = 56 * 1024 * 1024

    links = (n_sec - 1) * PIECES
    packs, both = pl.pallas_call(
        functools.partial(spread_kernel, n_sec, n_s),
        out_shape=(
            shape((GROUP, pool, reduced + tangents), f32),
            shape((n_sec, reduced, cols), bf16),
        ),
        in_specs=[pl.BlockSpec(memory_space=pltpu.SMEM), VMEM, VMEM, ANY],
        out_specs=(VMEM, VMEM),
        scratch_shapes=[dma(GROUP - 1), dma(GROUP - 1), dma(links), dma(links),
                        dma(links), dma(links), pltpu.SemaphoreType.DMA],
        compiler_params=pltpu.CompilerParams(
            collective_id=0, has_side_effects=True, vmem_limit_bytes=limit
        ),
        name="spread",
    )(plan, samples, directions, weights)

    per = lambda *s: pl.BlockSpec((1,) + s, lambda i, *_: (i,) + (0,) * len(s))
    all_of = lambda *s: pl.BlockSpec(s, lambda i, *_: (0,) * len(s))
    sample = lambda i: jnp.minimum(i, spt - 1)
    act, picked, slopes, partial, jac_target, target = pl.pallas_call(
        functools.partial(forward_kernel, spt),
        out_shape=(
            shape((team, high, cols), bf16),
            shape((team, rows, cols), bf16),
            shape((team, 2 * PAD, cols), f32),
            shape((team, high, reduced), bf16),
            shape((spt, tangents, reduced), bf16),
            shape((PAD, reduced), bf16),
        ),
        grid_spec=pltpu.PrefetchScalarGridSpec(
            num_scalar_prefetch=2,
            grid=(team,),
            in_specs=[
                all_of(*packs.shape),
                all_of(*both.shape),
                pl.BlockSpec(
                    (1, tangents, reduced),
                    lambda i, plan, sec: (plan[0, sec[0] * spt + sample(i)], 0, 0),
                ),
                all_of(*targets.shape),
            ],
            out_specs=(
                per(high, cols), per(rows, cols), per(2 * PAD, cols), per(high, reduced),
                pl.BlockSpec((1, tangents, reduced), lambda i, *_: (sample(i), 0, 0)),
                all_of(PAD, reduced),
            ),
        ),
        compiler_params=pltpu.CompilerParams(vmem_limit_bytes=limit),
        name="forward",
    )(plan, sec.reshape(1), packs, both, jacobian_targets, targets)

    quads = team // 2
    kinds = 3 if n_s == 4 else n_s - 1
    slab = reduced // n_s
    vmem = pltpu.VMEM
    result = pl.pallas_call(
        functools.partial(step_kernel, n_sec, n_s, spt),
        out_shape=shape((reduced // n_dp, width), f32),
        in_specs=[VMEM] * 5 + [ANY] * 3,
        out_specs=VMEM,
        scratch_shapes=[
            vmem((quads, high, reduced), bf16),
            vmem((quads - 1, high, reduced), bf16),
            vmem((quads - 1, high, reduced), bf16),
            vmem((team, high, reduced), bf16),
            vmem(act.shape, bf16),
            vmem(picked.shape, bf16),
            vmem(slopes.shape, f32),
            vmem((n_sec, reduced, cols), f32),
            vmem((n_sec, reduced, cols), bf16),
            vmem((team * PAD, cols), bf16),
            vmem((team * PAD, reduced), bf16),
            vmem((n_sec, kinds, slab, cols), bf16),
            vmem((n_sec, slab, cols), bf16),
            vmem((team, reduced // n_dp, cols), f32),
            dma(quads), dma(quads), dma(quads - 1), dma(quads - 1),
            dma(quads - 1), dma(quads - 1), dma(quads), dma(quads),
            dma(n_sec * kinds), dma(n_sec * kinds), dma(team), dma(team),
            dma(3), pltpu.SemaphoreType.DMA,
        ],
        compiler_params=pltpu.CompilerParams(
            collective_id=1, has_side_effects=True, vmem_limit_bytes=limit
        ),
        name="step",
    )(partial, jac_target, target, packs, both, act, picked, slopes)
    return result[None]


def solution(mesh):
    placed = (
        P("dp", None),
        P("dp", None),
        P("dp", None, None),
        P("dp", None),
        P("dp", None),
        P("section", None, None),
    )
    body = functools.partial(shards, mesh.shape["dp"], mesh.shape["section"])
    return jax.shard_map(
        body, mesh=mesh, in_specs=placed, out_specs=P("section", "dp", None), check_vma=False
    )
```

profile of v0, /device:TPU:0, one launch (start us, length us, event | category | flops | bytes accessed | tf_op | source)
XLA Modules:
  0.0 123.5 jit_solution(10814785876123600494)
XLA Ops:
  0.0 24.3 %spread.1 = (f32[4,8,640]{2,1,0:T(8,128)}, bf16[2,512,1024]{2,1,0:T(8,128)(2,1)}) custom-call(s32[1,8]{1,0:T(1,128)} %plan.3, bf16[8,512]{1,0:T(8,128)(2,1)} %samples.1, s32[8,128]{1,0:T(8,128)} %directions.1, bf16[1,512,8192]{2,1,0:T(8,128)(2,1)} %weight.1), custom_call_target="tpu_custom_call" | custom-call | tf_op jit(solution)/shard_map/spread/pallas_call | solution.py:436
  24.3 11.2 %forward.1 = (bf16[8,272,1024]{2,1,0:T(8,128)(2,1)}, bf16[8,256,1024]{2,1,0:T(8,128)(2,1)}, f32[8,32,1024]{2,1,0:T(8,128)}, bf16[8,272,512]{2,1,0:T(8,128)(2,1)}...) custom-call(s32[1,8]{1,0:T(1,128)} %plan.3, s32[1]{0:T(128)} %bitcast.sec, f32[4,8,640]{2,1,0:T(8,128)} %get-tuple-element.13.packs, ...), custom_call_target="tpu_custom_call" | custom-call | tf_op jit(solution)/shard_map/forward/pallas_call | solution.py:455
  35.6 85.6 %step.1 = f32[32,8192]{1,0:T(8,128)} custom-call(bf16[8,272,512]{2,1,0:T(8,128)(2,1)} %get-tuple-element.15.partial, bf16[2,128,512]{2,1,0:T(8,128)(2,1)} %get-tuple-element.16.jac_target, bf16[16,512]{1,0:T(8,128)(2,1)} %get-tuple-element.17.target, f32[4,8,640]{2,1,0:T(8,128)} %get-tuple-element.13.packs, bf16[2,512,1024]{2,1,0:T(8,128)(2,1)} %get-tuple-element.14.both, ...), custom_call_target="tpu_custom_call" | custom-call | tf_op jit(solution)/shard_map/step/pallas_call | solution.py:491
  121.2 2.3 %copy.8 = f32[1,32,8192]{2,1,0:T(8,128)} copy(f32[1,32,8192]{2,1,0:T(8,128)} %bitcast.2) | data formatting | bytes 2097152
where the time goes:
time: 124 us; the launch traced here: 123 us
  Pallas kernels  121 us (98%)
  local copies, waits for them, and re-layouts  2.26 us (2%)
    pallas_call x1, Pallas kernels, shards(): pl.pallas_call(functools.partial(step_kernel, n_sec, n_s, spt), out_shape...  85.6 us
    pallas_call x1, Pallas kernels, shards(): pl.pallas_call(functools.partial(spread_kernel, n_sec, n_s), out_shape=(s...  24.3 us
    pallas_call x1, Pallas kernels, shards(): pl.pallas_call(functools.partial(forward_kernel, spt), out_shape=(shape((...  11.2 us

commit v1 on v0

v1 whole, which is shorter than its diff:
```python
import functools

import jax
import jax.numpy as jnp
from jax import lax
from jax.experimental import pallas as pl
from jax.experimental.pallas import tpu as pltpu
from jax.sharding import PartitionSpec as P

MICRO = 4
GROUP = 4
PAD = 16
PIECES = 8
CHUNKS = 4
STRIPS = 4
QUADS = 4

jacobian_weight = 32.0

VMEM = pl.BlockSpec(memory_space=pltpu.VMEM)
ANY = pl.BlockSpec(memory_space=pl.ANY)


def remote(src, dst, send, recv, dp, sec):
    return pltpu.make_async_remote_copy(
        src_ref=src, dst_ref=dst, send_sem=send, recv_sem=recv,
        device_id={"dp": dp, "section": sec},
    )


def fused_kernel(
    n_s, plan, samples, directions, targets, jac_hbm, weight, out,
    packs, both, jac, xs, dirs, onehot_t, onehot, act, hidden, picked, first, second,
    partial, first_in, sums, second_in, misfit, total, grads, inbox, halves,
    last_total, last_grads, last_inbox, last_halves, pulled, proj, finished,
    psend, precv, wsend, wrecv, zsend, zrecv, s1, r1, s2, r2, s3, r3, s4, r4,
    s5, r5, s6, r6, s7, r7, local,
):
    f32, bf16 = jnp.float32, jnp.bfloat16
    dp, sec = lax.axis_index("dp"), lax.axis_index("section")
    g = lax.rem(dp, GROUP)
    base = dp - g
    s = dp // GROUP
    core, half = lax.rem(g, 2), g // 2
    q = sec * 2 + half
    mine = core * QUADS + q
    partner = (base + half * 2 + (1 - core), sec)
    parity = lax.rem(s, 2)
    mate = s + 1 - 2 * parity
    twin = (mate * GROUP + g, sec)
    line = n_s == 4
    reduced, cols = both.shape[1:]
    tangents = directions.shape[1]
    spt = MICRO // 2
    rows = spt * tangents
    strip = reduced // STRIPS
    slab = reduced // n_s
    own_rows = slab // GROUP
    cw = cols // CHUNKS
    pw = cols // PIECES
    over_rows = (((0,), (0,)), ((), ()))
    over_cols = (((1,), (1,)), ((), ()))

    def quad(k):
        l = 1 - sec if k & 2 else sec
        h = 1 - half if k & 1 else half
        return l * 2 + h, (base + h * 2 + core, l)

    if line:
        opposite = lax.rem(s + 2, 4)
        mate_opposite = lax.rem(mate + 2, 4)
        others = [mate, opposite]
        order = [mate_opposite, opposite, mate, s]
        pairs = [1 - s // 2, s // 2]
    else:
        others = [lax.rem(s + k, n_s) for k in range(1, n_s)]
        order = list(range(STRIPS))
        pairs = [0, 1]

    own = pltpu.make_async_copy(
        weight.at[0, :, pl.ds(pl.multiple_of((sec * GROUP + g) * cols, cols), cols)],
        both.at[sec], local.at[0],
    )
    own.start()
    load_jac = pltpu.make_async_copy(jac_hbm, jac, local.at[1])
    load_jac.start()

    barrier = pltpu.get_barrier_semaphore()
    peers = [
        (base + lax.rem(g + k, GROUP), 1 - sec if j else sec)
        for j in range(2) for k in range(GROUP) if j or k
    ] + [(o * GROUP + g, sec) for o in others]
    for d, l in peers:
        pl.semaphore_signal(barrier, inc=1, device_id={"dp": d, "section": l})
    pl.semaphore_wait(barrier, len(peers))

    half_rows = pl.ds(pl.multiple_of(parity * (reduced // 2), reduced // 2), reduced // 2)
    far_start = pl.multiple_of(((1 - sec) * GROUP + g) * cols, cols)
    sent, relayed = [], []
    for c in range(PIECES):
        sent.append(remote(
            weight.at[0, half_rows, pl.ds(far_start + c * pw, pw)],
            both.at[sec, half_rows, pl.ds(c * pw, pw)],
            wsend.at[c], wrecv.at[c], dp, 1 - sec,
        ))
        sent[-1].start()

    every = jnp.concatenate(
        [samples[...].astype(f32), directions[...].astype(f32)], axis=1
    )
    row = lax.broadcasted_iota(jnp.int32, every.shape, 0)
    packed = jnp.zeros_like(every)
    for k in range(MICRO):
        chosen = jnp.sum(jnp.where(row == plan[0, k], every, 0.0), axis=0, keepdims=True)
        packed = jnp.where(row == k, chosen, packed)
    packs[g] = packed
    shared = []
    for k in range(1, GROUP):
        shared.append(remote(
            packs.at[g], packs.at[g], psend.at[k - 1], precv.at[k - 1],
            base + lax.rem(g + k, GROUP), sec,
        ))
        shared[-1].start()
    for copy in shared:
        copy.wait_recv()
    for b in range(2 * QUADS):
        c, l, h = b // QUADS, (b % QUADS) // 2, b % 2
        xs[b * spt : (b + 1) * spt] = packs[h * 2 + c, l * spt : (l + 1) * spt, :reduced]
        dirs[b * spt : (b + 1) * spt] = packs[h * 2 + c, l * spt : (l + 1) * spt, reduced:]
    n_all = 2 * QUADS * spt
    turned = dirs[...].T
    for t in range(n_all):
        lane = lax.broadcasted_iota(jnp.int32, (tangents, reduced), 1).astype(f32)
        onehot_t[t * tangents : (t + 1) * tangents] = (
            (lane == turned[:, t : t + 1]).astype(f32).astype(bf16)
        )

    n_loop = 2
    loop_rows = n_all * tangents // n_loop
    loop_samples = n_all // n_loop

    def forward(c):
        lo, hi = c * cw, (c + 1) * cw
        linear = jnp.dot(xs[...].astype(bf16), both[0, :, lo:hi], preferred_element_type=f32)
        squash = jax.nn.sigmoid(linear)
        first[:, lo:hi] = squash * (1.0 + linear * (1.0 - squash))
        second[:, lo:hi] = squash * (1.0 - squash) * (2.0 + linear * (1.0 - 2.0 * squash))
        hidden[:, lo:hi] = (linear * squash).astype(bf16)

        def pick(i, carry):
            start = pl.multiple_of(i * loop_rows, loop_rows)
            value = jnp.dot(
                onehot_t[pl.ds(start, loop_rows), :], both[0, :, lo:hi],
                preferred_element_type=f32,
            )
            picked[pl.ds(start, loop_rows), lo:hi] = value.astype(bf16)
            for t in range(loop_samples):
                slope = first[pl.ds(i * loop_samples + t, 1), lo:hi]
                here = pl.ds(pl.multiple_of(start + t * tangents, tangents), tangents)
                act[here, lo:hi] = (
                    slope * value[t * tangents : (t + 1) * tangents]
                ).astype(bf16)
            return carry

        lax.fori_loop(0, n_loop, pick, 0)

    own.wait()
    per_chunk = PIECES // CHUNKS

    def arrive(c):
        for i in range(c * per_chunk, (c + 1) * per_chunk):
            sent[i].wait_recv()
            came = both.at[1 - sec, half_rows, pl.ds(i * pw, pw)]
            relayed.append(remote(came, came, zsend.at[i], zrecv.at[i], *twin))
            relayed[-1].start()

    def complete(c):
        for i in range(c * per_chunk, (c + 1) * per_chunk):
            relayed[i].wait_recv()

    for c in range(CHUNKS):
        arrive(c)
        if c:
            complete(c - 1)
            forward(c - 1)
    complete(CHUNKS - 1)
    forward(CHUNKS - 1)

    def partials(pair, side):
        start = pl.multiple_of(pair * 2 * strip, 2 * strip)
        decoder = both[1, pl.ds(start, 2 * strip), :]
        lo = pl.multiple_of(side * (QUADS * rows), QUADS * rows)
        value = lax.dot_general(
            act[pl.ds(lo, QUADS * rows), :], decoder, over_cols, preferred_element_type=f32
        ).astype(bf16)
        tail = lax.dot_general(
            hidden[...], decoder, over_cols, preferred_element_type=f32
        ).astype(bf16)
        for i in range(2):
            a, b = i * strip, (i + 1) * strip
            for j in range(QUADS):
                partial[pair * 2 + i, side * QUADS + j, 0:rows] = (
                    value[j * rows : (j + 1) * rows, a:b]
                )
                partial[pair * 2 + i, side * QUADS + j, rows:] = tail[:, a:b]

    def across(p):
        theirs = pl.ds(pl.multiple_of((1 - core) * QUADS, QUADS), QUADS)
        return remote(
            partial.at[p, theirs], first_in.at[p], s1.at[p], r1.at[p], *partner
        )

    def away(p, k):
        return remote(
            sums.at[p, k - 1], second_in.at[p, k - 1],
            s2.at[p * 3 + k - 1], r2.at[p * 3 + k - 1], *quad(k)[1],
        )

    def gather(p, k):
        if k == 0:
            return remote(
                misfit.at[p, mine], misfit.at[p, mine], s4.at[p * 4], r4.at[p * 4], *partner
            )
        return remote(
            misfit.at[p, mine], misfit.at[p, mine],
            s3.at[p * 3 + k - 1], r3.at[p * 3 + k - 1], *quad(k)[1],
        )

    def passing(p, k):
        came = misfit.at[p, core * QUADS + quad(k)[0]]
        return remote(came, came, s4.at[p * 4 + k], r4.at[p * 4 + k], *partner)

    def reduce_out(p):
        across(p).wait_recv()
        for k in (3, 1, 2):
            other = quad(k)[0]
            sums[p, k - 1] = (
                partial[p, core * QUADS + other].astype(f32) + first_in[p, other].astype(f32)
            ).astype(bf16)
            away(p, k).start()

    def compare(p):
        for k in range(1, QUADS):
            away(p, k).wait_recv()
        lanes = pl.ds(pl.multiple_of(p * strip, strip), strip)

        def whole(lo, hi):
            value = partial[p, mine, lo:hi].astype(f32) + first_in[p, q, lo:hi].astype(f32)
            for k in range(1, QUADS):
                value = value + second_in[p, k - 1, lo:hi].astype(f32)
            return value

        all_targets = targets[:, lanes].astype(f32)
        pool_row = lax.broadcasted_iota(jnp.int32, all_targets.shape, 0)
        tail_row = lax.broadcasted_iota(jnp.int32, (PAD, strip), 0)
        tail = jnp.zeros((PAD, strip), f32)
        outputs = whole(rows, rows + PAD)
        for i in range(spt):
            lo, hi = i * tangents, (i + 1) * tangents
            index = plan[0, sec * spt + i]
            misfit[p, mine, lo:hi] = (
                jacobian_weight * (whole(lo, hi) - jac[index, :, lanes].astype(f32))
            ).astype(bf16)
            target = jnp.sum(
                jnp.where(pool_row == index, all_targets, 0.0), axis=0, keepdims=True
            )
            tail = jnp.where(tail_row == mine * spt + i, outputs - target, tail)
        misfit[p, mine, rows:] = tail.astype(bf16)
        for k in (3, 1, 2, 0):
            gather(p, k).start()

    def pass_on(p):
        for k in (1, 2, 3):
            gather(p, k).wait_recv()
            passing(p, k).start()

    def last_of(p):
        for k in range(QUADS):
            (passing(p, k) if k else gather(p, 0)).wait_recv()
        lhs = jnp.concatenate([misfit[p, b, 0:rows] for b in range(2 * QUADS)], axis=0)
        value = lax.dot_general(lhs, act[...], over_rows, preferred_element_type=f32)
        tail = misfit[p, 0, rows:].astype(f32)
        for b in range(1, 2 * QUADS):
            tail = tail + misfit[p, b, rows:].astype(f32)
        value = value + lax.dot_general(
            tail.astype(bf16), hidden[...], over_rows, preferred_element_type=f32
        )
        here = pl.ds(pl.multiple_of(p * strip, strip), strip)
        last_total[here, :] = value
        last_grads[here, :] = value.astype(bf16)

    def slab_of(o):
        return pl.ds(pl.multiple_of(o * slab, slab), slab)

    def last_link(kind):
        if not line:
            o = others[kind]
            source = last_grads.at[slab_of(o), :]
        elif kind == 2:
            o, source = opposite, last_halves
        else:
            o, source = mate, last_grads.at[slab_of([mate_opposite, mate][kind]), :]
        return remote(
            source, last_inbox.at[kind], s5.at[kind], r5.at[kind], o * GROUP + g, sec
        )

    def last_relay():
        last_link(0).wait_recv()
        last_halves[...] = (
            last_total[slab_of(opposite), :] + last_inbox[0].astype(f32)
        ).astype(bf16)
        last_link(2).start()

    def link(j, kind):
        if not line:
            o = others[kind]
            source = grads.at[j, slab_of(o), :]
        elif kind == 2:
            o, source = opposite, halves.at[j]
        else:
            o, source = mate, grads.at[j, slab_of([mate_opposite, mate][kind]), :]
        i = j * inbox.shape[1] + kind
        return remote(source, inbox.at[j, kind], s6.at[i], r6.at[i], o * GROUP + g, sec)

    def relay(j):
        link(j, 0).wait_recv()
        halves[j] = (
            total[j, slab_of(opposite), :] + inbox[j, 0].astype(f32)
        ).astype(bf16)
        link(j, 2).start()

    def columns(j):
        start = pl.multiple_of((sec * GROUP + g) * cols + j * cw, cw)
        return out.at[:, pl.ds(start, cw)]

    def hand(layer, j, k):
        h = lax.rem(g + k, GROUP)
        i = j * 2 * GROUP
        return remote(
            finished.at[layer, j, h], columns(j),
            s7.at[layer * CHUNKS * GROUP + j * GROUP + k], r7.at[i + sec * GROUP + k],
            base + h, layer,
        )

    kinds = range(1, 3) if line else range(n_s - 1)

    def finish(layer, j):
        for h in range(GROUP):
            start = pl.multiple_of(s * slab + h * own_rows, own_rows)
            here = slice(h * own_rows, (h + 1) * own_rows)
            if layer:
                lo, hi = j * cw, (j + 1) * cw
                value = last_total[pl.ds(start, own_rows), lo:hi]
                for k in kinds:
                    value = value + last_inbox[k, here, lo:hi].astype(f32)
            else:
                value = total[j, pl.ds(start, own_rows), :]
                for k in kinds:
                    value = value + inbox[j, k, here, :].astype(f32)
            finished[layer, j, h] = value.astype(bf16)
        for k in range(1, GROUP):
            hand(layer, j, k).start()

        @pl.when(sec != layer)
        def _():
            hand(layer, j, 0).start()

        @pl.when(sec == layer)
        def _():
            columns(j)[...] = finished[layer, j, g]

    def backward(j):
        lo, hi = j * cw, (j + 1) * cw

        def pull(i, carry):
            lhs = jnp.concatenate(
                [
                    jnp.concatenate(
                        [misfit[p, i * QUADS + b, 0:rows] for p in range(STRIPS)], axis=1
                    )
                    for b in range(QUADS)
                ],
                axis=0,
            )
            cot = jnp.dot(lhs, both[1, :, lo:hi], preferred_element_type=f32)
            start = pl.multiple_of(i * loop_rows, loop_rows)
            for t in range(loop_samples):
                part = cot[t * tangents : (t + 1) * tangents]
                here = pl.ds(pl.multiple_of(start + t * tangents, tangents), tangents)
                slope = first[pl.ds(i * loop_samples + t, 1), lo:hi]
                proj[pl.ds(i * loop_samples + t, 1), :] = jnp.sum(
                    part * picked[here, lo:hi].astype(f32), axis=0, keepdims=True
                )
                pulled[here, :] = (part * slope).astype(bf16)
            return carry

        lax.fori_loop(0, n_loop, pull, 0)
        tail = jnp.zeros((PAD, reduced), f32)
        for b in range(2 * QUADS):
            tail = tail + jnp.concatenate(
                [misfit[p, b, rows:] for p in range(STRIPS)], axis=1
            ).astype(f32)
        cot = jnp.dot(tail.astype(bf16), both[1, :, lo:hi], preferred_element_type=f32)
        pre = (cot * first[:, lo:hi] + second[:, lo:hi] * proj[...]).astype(bf16)
        value = jnp.dot(onehot[...], pulled[...], preferred_element_type=f32)
        value = value + lax.dot_general(
            xs[...].astype(bf16), pre, over_rows, preferred_element_type=f32
        )
        total[j] = value
        grads[j] = value.astype(bf16)

    for i in range(2):
        partials(pairs[i], 1 - core)
        across(order[2 * i]).start()
        across(order[2 * i + 1]).start()
        partials(pairs[i], core)
    reduce_out(order[0])
    reduce_out(order[1])
    for t in range(n_all):
        deep = lax.broadcasted_iota(jnp.int32, (reduced, tangents), 0).astype(f32)
        onehot[:, t * tangents : (t + 1) * tangents] = (
            (deep == dirs[t : t + 1, :]).astype(f32).astype(bf16)
        )
    load_jac.wait()
    compare(order[0])
    reduce_out(order[2])
    compare(order[1])
    reduce_out(order[3])
    pass_on(order[0])
    compare(order[2])
    last_of(order[0])
    if line:
        last_link(0).start()
    pass_on(order[1])
    compare(order[3])
    last_of(order[1])
    pass_on(order[2])
    if line:
        last_relay()
    last_of(order[2])
    if line:
        last_link(1).start()
    pass_on(order[3])
    if line:
        for k in range(QUADS):
            (passing(order[3], k) if k else gather(order[3], 0)).wait_recv()
    else:
        last_of(order[3])
        for kind in range(n_s - 1):
            last_link(kind).start()
    for j in range(CHUNKS):
        backward(j)
        if line:
            link(j, 0).start()
            link(j, 1).start()
            if j >= 2:
                relay(j - 2)
        else:
            for kind in range(n_s - 1):
                link(j, kind).start()
    if line:
        relay(CHUNKS - 2)
        lhs = jnp.concatenate(
            [misfit[order[3], b, 0:rows] for b in range(2 * QUADS)], axis=0
        )
        value = lax.dot_general(lhs, act[...], over_rows, preferred_element_type=f32)
        tail = misfit[order[3], 0, rows:].astype(f32)
        for b in range(1, 2 * QUADS):
            tail = tail + misfit[order[3], b, rows:].astype(f32)
        last_total[slab_of(s), :] = value + lax.dot_general(
            tail.astype(bf16), hidden[...], over_rows, preferred_element_type=f32
        )
        relay(CHUNKS - 1)
    for k in kinds:
        last_link(k).wait_recv()
    for j in range(CHUNKS):
        finish(1, j)
    for j in range(CHUNKS):
        for k in kinds:
            link(j, k).wait_recv()
        finish(0, j)

    for copy in shared + sent + relayed:
        copy.wait_send()
    for p in range(STRIPS):
        across(p).wait_send()
        for k in range(1, QUADS):
            away(p, k).wait_send()
            passing(p, k).wait_send()
        for k in range(QUADS):
            gather(p, k).wait_send()
    for k in range(last_inbox.shape[0]):
        last_link(k).wait_send()
        for j in range(CHUNKS):
            link(j, k).wait_send()
    for layer in range(2):
        for j in range(CHUNKS):
            for k in range(1, GROUP):
                hand(layer, j, k).wait_send()

            @pl.when(sec != layer)
            def _():
                hand(layer, j, 0).wait_send()

    for j in range(CHUNKS):
        for i in range(2):
            for k in range(GROUP):
                at = j * 2 * GROUP + i * GROUP + k
                arrival = remote(
                    finished.at[0, j, 0], columns(j), s7.at[0], r7.at[at], *partner
                )
                if k:
                    arrival.wait_recv()
                else:

                    @pl.when(sec != i)
                    def _():
                        arrival.wait_recv()


def shards(n_dp, n_sec, samples, targets, jacobian_targets, directions, plan, weights):
    _, reduced, width = weights.shape
    pool, tangents = directions.shape
    team = n_sec * GROUP
    cols = width // team
    n_s = n_dp // GROUP
    spt = MICRO // n_sec
    rows = spt * tangents
    high = rows + PAD
    every = team * spt
    strip = reduced // STRIPS
    slab = reduced // n_s
    cw = cols // CHUNKS
    kinds = 3 if n_s == 4 else n_s - 1
    f32, bf16 = jnp.float32, jnp.bfloat16
    vmem = pltpu.VMEM
    dma = lambda n: pltpu.SemaphoreType.DMA((n,))
    result = pl.pallas_call(
        functools.partial(fused_kernel, n_s),
        out_shape=jax.ShapeDtypeStruct((reduced // n_dp, width), bf16),
        in_specs=[pl.BlockSpec(memory_space=pltpu.SMEM), VMEM, VMEM, VMEM, ANY, ANY],
        out_specs=VMEM,
        scratch_shapes=[
            vmem((GROUP, pool, reduced + tangents), f32),
            vmem((n_sec, reduced, cols), bf16),
            vmem(jacobian_targets.shape, bf16),
            vmem((every, reduced), f32),
            vmem((every, tangents), f32),
            vmem((every * tangents, reduced), bf16),
            vmem((reduced, every * tangents), bf16),
            vmem((every * tangents, cols), bf16),
            vmem((every, cols), bf16),
            vmem((every * tangents, cols), bf16),
            vmem((every, cols), f32),
            vmem((every, cols), f32),
            vmem((STRIPS, team, high, strip), bf16),
            vmem((STRIPS, QUADS, high, strip), bf16),
            vmem((STRIPS, QUADS - 1, high, strip), bf16),
            vmem((STRIPS, QUADS - 1, high, strip), bf16),
            vmem((STRIPS, team, high, strip), bf16),
            vmem((CHUNKS, reduced, cw), f32),
            vmem((CHUNKS, reduced, cw), bf16),
            vmem((CHUNKS, kinds, slab, cw), bf16),
            vmem((CHUNKS, slab, cw), bf16),
            vmem((reduced, cols), f32),
            vmem((reduced, cols), bf16),
            vmem((kinds, slab, cols), bf16),
            vmem((slab, cols), bf16),
            vmem((every * tangents, cw), bf16),
            vmem((every, cw), f32),
            vmem((n_sec, CHUNKS, GROUP, reduced // n_dp, cw), bf16),
            dma(GROUP - 1), dma(GROUP - 1), dma(PIECES), dma(PIECES), dma(PIECES), dma(PIECES),
            dma(STRIPS), dma(STRIPS), dma(STRIPS * 3), dma(STRIPS * 3),
            dma(STRIPS * 3), dma(STRIPS * 3), dma(STRIPS * 4), dma(STRIPS * 4),
            dma(kinds), dma(kinds), dma(CHUNKS * kinds), dma(CHUNKS * kinds),
            dma(2 * CHUNKS * GROUP), dma(2 * CHUNKS * GROUP), dma(2),
        ],
        compiler_params=pltpu.CompilerParams(
            collective_id=0, has_side_effects=True, vmem_limit_bytes=60 * 1024 * 1024
        ),
        name="fused",
    )(plan, samples, directions, targets, jacobian_targets, weights)
    return result.astype(f32)[None]


def solution(mesh):
    placed = (
        P("dp", None),
        P("dp", None),
        P("dp", None, None),
        P("dp", None),
        P("dp", None),
        P("section", None, None),
    )
    body = functools.partial(shards, mesh.shape["dp"], mesh.shape["section"])
    return jax.shard_map(
        body, mesh=mesh, in_specs=placed, out_specs=P("section", "dp", None), check_vma=False
    )
```

time: 124 us -> 94.6 us (0.76)
  Pallas kernels: 121 us -> 92.3 us
  local copies, waits for them, and re-layouts: 2.26 us -> 0 us
  other arithmetic: 0 us -> 2.08 us
    pallas_call x3 -> x1, Pallas kernels: 121 us -> 92.3 us  [shards(): pl.pallas_call(functools.partial(fused_kernel, n_s), out_shape=jax.ShapeD...]
    unnamed x1 -> x0, local copies, waits for them, and re-layouts: 2.26 us -> none
    broadcast_in_dim x0 -> x1, other arithmetic: none -> 2.08 us  [shards(): return result.astype(f32)[None]]
where the time goes in v1:
time: 94.6 us; the launch traced here: 94.4 us
  Pallas kernels  92.3 us (98%)
  other arithmetic  2.08 us (2%)
    pallas_call x1, Pallas kernels, shards(): pl.pallas_call(functools.partial(fused_kernel, n_s), out_shape=jax.ShapeD...  92.3 us
    broadcast_in_dim x1, other arithmetic, shards(): return result.astype(f32)[None]  2.08 us

profile of v1, /device:TPU:0, one launch (start us, length us, event | category | flops | bytes accessed | tf_op | source)
XLA Modules:
  0.0 94.4 jit_solution(8558454642251039058)
XLA Ops:
  0.0 92.3 %fused.1 = bf16[32,8192]{1,0:T(8,128)(2,1)} custom-call(s32[1,8]{1,0:T(1,128)} %plan.1, bf16[8,512]{1,0:T(8,128)(2,1)} %samples.1, s32[8,128]{1,0:T(8,128)} %directions.1, bf16[8,512]{1,0:T(8,128)(2,1)} %targets.1, bf16[8,128,512]{2,1,0:T(8,128)(2,1)} %jac_hbm.1, bf16[1,512,8192]{2,1,0:T(8,128)(2,1)} %weight.1), custom_call_target="tpu_custom_call" | custom-call | tf_op jit(solution)/shard_map/fused/pallas_call | solution.py:538
  92.4 2.1 %bitcast_convert_fusion = f32[1,32,8192]{2,1,0:T(8,128)} fusion(bf16[32,8192]{1,0:T(8,128)(2,1)} %fused.1), kind=kLoop, calls=%fused_computation | loop fusion | flops 262144 | bytes 1572864 | tf_op jit(solution)/shard_map/broadcast_in_dim | solution.py:583

commit v2 on v1

--- a/solution.py
+++ b/solution.py
@@ -13,6 +13,8 @@
 PIECES = 8
 CHUNKS = 4
 STRIPS = 4
+LINKS = 8
+LASTS = 2
 QUADS = 4
 
 jacobian_weight = 32.0
@@ -30,7 +32,7 @@
 
 def fused_kernel(
     n_s, plan, samples, directions, targets, jac_hbm, weight, out,
-    packs, both, jac, xs, dirs, onehot_t, onehot, act, hidden, picked, first, second,
+    packs, both, mail, jac, xs, dirs, onehot_t, onehot, act, hidden, picked, first, second,
     partial, first_in, sums, second_in, misfit, total, grads, inbox, halves,
     last_total, last_grads, last_inbox, last_halves, pulled, proj, finished,
     psend, precv, wsend, wrecv, zsend, zrecv, s1, r1, s2, r2, s3, r3, s4, r4,
@@ -58,6 +60,8 @@
     own_rows = slab // GROUP
     cw = cols // CHUNKS
     pw = cols // PIECES
+    zw = cols // LINKS
+    lw = cols // LASTS
     over_rows = (((0,), (0,)), ((), ()))
     over_cols = (((1,), (1,)), ((), ()))
 
@@ -77,6 +81,11 @@
         order = list(range(STRIPS))
         pairs = [0, 1]
 
+    far_start = pl.multiple_of(((1 - sec) * GROUP + g) * cols, cols)
+    load_mail = pltpu.make_async_copy(
+        weight.at[0, :, pl.ds(far_start, cols)], mail, local.at[2]
+    )
+    load_mail.start()
     own = pltpu.make_async_copy(
         weight.at[0, :, pl.ds(pl.multiple_of((sec * GROUP + g) * cols, cols), cols)],
         both.at[sec], local.at[0],
@@ -94,14 +103,15 @@
         pl.semaphore_signal(barrier, inc=1, device_id={"dp": d, "section": l})
     pl.semaphore_wait(barrier, len(peers))
 
-    half_rows = pl.ds(pl.multiple_of(parity * (reduced // 2), reduced // 2), reduced // 2)
-    far_start = pl.multiple_of(((1 - sec) * GROUP + g) * cols, cols)
+    side = reduced // 2
+    half_rows = pl.ds(pl.multiple_of(parity * side, side), side)
+    other_rows = pl.ds(pl.multiple_of((1 - parity) * side, side), side)
+    load_mail.wait()
     sent, relayed = [], []
-    for c in range(PIECES):
+    for c in range(PIECES + 1):
+        here = (half_rows if c < PIECES else other_rows, pl.ds(min(c, PIECES - 1) * pw, pw))
         sent.append(remote(
-            weight.at[0, half_rows, pl.ds(far_start + c * pw, pw)],
-            both.at[sec, half_rows, pl.ds(c * pw, pw)],
-            wsend.at[c], wrecv.at[c], dp, 1 - sec,
+            mail.at[here], both.at[(sec,) + here], wsend.at[c], wrecv.at[c], dp, 1 - sec,
         ))
         sent[-1].start()
 
@@ -121,6 +131,15 @@
             base + lax.rem(g + k, GROUP), sec,
         ))
         shared[-1].start()
+
+    def arrive(c):
+        sent[c].wait_recv()
+        if c < PIECES - 1:
+            came = both.at[1 - sec, half_rows, pl.ds(c * pw, pw)]
+            relayed.append(remote(came, came, zsend.at[c], zrecv.at[c], *twin))
+            relayed[-1].start()
+
+    arrive(0)
     for copy in shared:
         copy.wait_recv()
     for b in range(2 * QUADS):
@@ -129,11 +148,19 @@
         dirs[b * spt : (b + 1) * spt] = packs[h * 2 + c, l * spt : (l + 1) * spt, reduced:]
     n_all = 2 * QUADS * spt
     turned = dirs[...].T
-    for t in range(n_all):
-        lane = lax.broadcasted_iota(jnp.int32, (tangents, reduced), 1).astype(f32)
-        onehot_t[t * tangents : (t + 1) * tangents] = (
-            (lane == turned[:, t : t + 1]).astype(f32).astype(bf16)
-        )
+
+    def spread_directions(ts):
+        for t in ts:
+            lane = lax.broadcasted_iota(jnp.int32, (tangents, reduced), 1).astype(f32)
+            onehot_t[t * tangents : (t + 1) * tangents] = (
+                (lane == turned[:, t : t + 1]).astype(f32).astype(bf16)
+            )
+
+    arrive(1)
+    spread_directions(range(n_all // 2))
+    arrive(2)
+    spread_directions(range(n_all // 2, n_all))
+    arrive(3)
 
     n_loop = 2
     loop_rows = n_all * tangents // n_loop
@@ -166,25 +193,12 @@
 
     own.wait()
     per_chunk = PIECES // CHUNKS
-
-    def arrive(c):
-        for i in range(c * per_chunk, (c + 1) * per_chunk):
-            sent[i].wait_recv()
-            came = both.at[1 - sec, half_rows, pl.ds(i * pw, pw)]
-            relayed.append(remote(came, came, zsend.at[i], zrecv.at[i], *twin))
-            relayed[-1].start()
-
-    def complete(c):
-        for i in range(c * per_chunk, (c + 1) * per_chunk):
+    for c in range(CHUNKS):
+        for i in ([], [4, 5], [6], [7, 8])[c]:
+            arrive(i)
+        for i in range(c * per_chunk, min((c + 1) * per_chunk, PIECES - 1)):
             relayed[i].wait_recv()
-
-    for c in range(CHUNKS):
-        arrive(c)
-        if c:
-            complete(c - 1)
-            forward(c - 1)
-    complete(CHUNKS - 1)
-    forward(CHUNKS - 1)
+        forward(c)
 
     def partials(pair, side):
         start = pl.multiple_of(pair * 2 * strip, 2 * strip)
@@ -292,24 +306,27 @@
     def slab_of(o):
         return pl.ds(pl.multiple_of(o * slab, slab), slab)
 
-    def last_link(kind):
+    def last_link(j, kind):
+        here = slice(j * lw, (j + 1) * lw)
         if not line:
             o = others[kind]
-            source = last_grads.at[slab_of(o), :]
+            source = last_grads.at[slab_of(o), here]
         elif kind == 2:
-            o, source = opposite, last_halves
+            o, source = opposite, last_halves.at[:, here]
         else:
-            o, source = mate, last_grads.at[slab_of([mate_opposite, mate][kind]), :]
+            o, source = mate, last_grads.at[slab_of([mate_opposite, mate][kind]), here]
+        i = j * last_inbox.shape[0] + kind
         return remote(
-            source, last_inbox.at[kind], s5.at[kind], r5.at[kind], o * GROUP + g, sec
-        )
-
-    def last_relay():
-        last_link(0).wait_recv()
-        last_halves[...] = (
-            last_total[slab_of(opposite), :] + last_inbox[0].astype(f32)
+            source, last_inbox.at[kind, :, here], s5.at[i], r5.at[i], o * GROUP + g, sec
+        )
+
+    def last_relay(j):
+        last_link(j, 0).wait_recv()
+        here = slice(j * lw, (j + 1) * lw)
+        last_halves[:, here] = (
+            last_total[slab_of(opposite), here] + last_inbox[0, :, here].astype(f32)
         ).astype(bf16)
-        last_link(2).start()
+        last_link(j, 2).start()
 
     def link(j, kind):
         if not line:
@@ -330,15 +347,15 @@
         link(j, 2).start()
 
     def columns(j):
-        start = pl.multiple_of((sec * GROUP + g) * cols + j * cw, cw)
-        return out.at[:, pl.ds(start, cw)]
+        start = pl.multiple_of((sec * GROUP + g) * cols + j * zw, zw)
+        return out.at[:, pl.ds(start, zw)]
 
     def hand(layer, j, k):
         h = lax.rem(g + k, GROUP)
         i = j * 2 * GROUP
         return remote(
             finished.at[layer, j, h], columns(j),
-            s7.at[layer * CHUNKS * GROUP + j * GROUP + k], r7.at[i + sec * GROUP + k],
+            s7.at[layer * LINKS * GROUP + j * GROUP + k], r7.at[i + sec * GROUP + k],
             base + h, layer,
         )
 
@@ -349,7 +366,7 @@
             start = pl.multiple_of(s * slab + h * own_rows, own_rows)
             here = slice(h * own_rows, (h + 1) * own_rows)
             if layer:
-                lo, hi = j * cw, (j + 1) * cw
+                lo, hi = j * zw, (j + 1) * zw
                 value = last_total[pl.ds(start, own_rows), lo:hi]
                 for k in kinds:
                     value = value + last_inbox[k, here, lo:hi].astype(f32)
@@ -368,6 +385,10 @@
         @pl.when(sec == layer)
         def _():
             columns(j)[...] = finished[layer, j, g]
+
+    def arrived(j):
+        for k in kinds:
+            link(j, k).wait_recv()
 
     def backward(j):
         lo, hi = j * cw, (j + 1) * cw
@@ -406,60 +427,11 @@
         value = value + lax.dot_general(
             xs[...].astype(bf16), pre, over_rows, preferred_element_type=f32
         )
-        total[j] = value
-        grads[j] = value.astype(bf16)
-
-    for i in range(2):
-        partials(pairs[i], 1 - core)
-        across(order[2 * i]).start()
-        across(order[2 * i + 1]).start()
-        partials(pairs[i], core)
-    reduce_out(order[0])
-    reduce_out(order[1])
-    for t in range(n_all):
-        deep = lax.broadcasted_iota(jnp.int32, (reduced, tangents), 0).astype(f32)
-        onehot[:, t * tangents : (t + 1) * tangents] = (
-            (deep == dirs[t : t + 1, :]).astype(f32).astype(bf16)
-        )
-    load_jac.wait()
-    compare(order[0])
-    reduce_out(order[2])
-    compare(order[1])
-    reduce_out(order[3])
-    pass_on(order[0])
-    compare(order[2])
-    last_of(order[0])
-    if line:
-        last_link(0).start()
-    pass_on(order[1])
-    compare(order[3])
-    last_of(order[1])
-    pass_on(order[2])
-    if line:
-        last_relay()
-    last_of(order[2])
-    if line:
-        last_link(1).start()
-    pass_on(order[3])
-    if line:
-        for k in range(QUADS):
-            (passing(order[3], k) if k else gather(order[3], 0)).wait_recv()
-    else:
-        last_of(order[3])
-        for kind in range(n_s - 1):
-            last_link(kind).start()
-    for j in range(CHUNKS):
-        backward(j)
-        if line:
-            link(j, 0).start()
-            link(j, 1).start()
-            if j >= 2:
-                relay(j - 2)
-        else:
-            for kind in range(n_s - 1):
-                link(j, kind).start()
-    if line:
-        relay(CHUNKS - 2)
+        for i in range(cw // zw):
+            total[j * (cw // zw) + i] = value[:, i * zw : (i + 1) * zw]
+            grads[j * (cw // zw) + i] = value[:, i * zw : (i + 1) * zw].astype(bf16)
+
+    def own_strip():
         lhs = jnp.concatenate(
             [misfit[order[3], b, 0:rows] for b in range(2 * QUADS)], axis=0
         )
@@ -470,15 +442,100 @@
         last_total[slab_of(s), :] = value + lax.dot_general(
             tail.astype(bf16), hidden[...], over_rows, preferred_element_type=f32
         )
-        relay(CHUNKS - 1)
-    for k in kinds:
-        last_link(k).wait_recv()
-    for j in range(CHUNKS):
-        finish(1, j)
-    for j in range(CHUNKS):
-        for k in kinds:
-            link(j, k).wait_recv()
-        finish(0, j)
+
+    def onehots():
+        for t in range(n_all):
+            deep = lax.broadcasted_iota(jnp.int32, (reduced, tangents), 0).astype(f32)
+            onehot[:, t * tangents : (t + 1) * tangents] = (
+                (deep == dirs[t : t + 1, :]).astype(f32).astype(bf16)
+            )
+
+    for i in range(2):
+        partials(pairs[i], 1 - core)
+        across(order[2 * i]).start()
+        across(order[2 * i + 1]).start()
+        partials(pairs[i], core)
+        if i == 0:
+            reduce_out(order[0])
+            reduce_out(order[1])
+    onehots()
+    load_jac.wait()
+    compare(order[0])
+    compare(order[1])
+    reduce_out(order[2])
+    reduce_out(order[3])
+    pass_on(order[0])
+    last_of(order[0])
+    if line:
+        for j in range(LASTS):
+            last_link(j, 0).start()
+    pass_on(order[1])
+    last_of(order[1])
+    compare(order[2])
+    if line:
+        last_relay(0)
+    compare(order[3])
+    if line:
+        for j in range(1, LASTS):
+            last_relay(j)
+    pass_on(order[2])
+    last_of(order[2])
+    if line:
+        for j in range(LASTS):
+            last_link(j, 1).start()
+    pass_on(order[3])
+    if line:
+        for k in range(QUADS):
+            (passing(order[3], k) if k else gather(order[3], 0)).wait_recv()
+        turns = [
+            ([0, 1], [], []), ([2, 3], [], [0, 1]), ([4, 5], [0, 1], [2, 3]),
+            ([6, 7], [2, 3], [4, 5]),
+        ]
+        for j, (out_first, through, out_second) in enumerate(turns):
+            backward(j)
+            for i in out_first:
+                link(i, 0).start()
+            for i in through:
+                relay(i)
+            for i in out_second:
+                link(i, 1).start()
+        own_strip()
+        relay(4)
+        relay(5)
+        link(6, 1).start()
+        link(7, 1).start()
+        for i in range(LASTS):
+            for k in kinds:
+                last_link(i, k).wait_recv()
+        for j in range(LINKS):
+            finish(1, j)
+        arrived(0)
+        finish(0, 0)
+        arrived(1)
+        finish(0, 1)
+        relay(6)
+        relay(7)
+        for j in range(2, LINKS):
+            arrived(j)
+            finish(0, j)
+    else:
+        last_of(order[3])
+        for kind in range(n_s - 1):
+            for j in range(LASTS):
+                last_link(j, kind).start()
+        for j in range(CHUNKS):
+            backward(j)
+            for kind in range(n_s - 1):
+                for i in range(j * LINKS // CHUNKS, (j + 1) * LINKS // CHUNKS):
+                    link(i, kind).start()
+        for i in range(LASTS):
+            for k in kinds:
+                last_link(i, k).wait_recv()
+        for j in range(LINKS):
+            finish(1, j)
+        for j in range(LINKS):
+            arrived(j)
+            finish(0, j)
 
     for copy in shared + sent + relayed:
         copy.wait_send()
@@ -490,11 +547,12 @@
         for k in range(QUADS):
             gather(p, k).wait_send()
     for k in range(last_inbox.shape[0]):
-        last_link(k).wait_send()
-        for j in range(CHUNKS):
+        for j in range(LASTS):
+            last_link(j, k).wait_send()
+        for j in range(LINKS):
             link(j, k).wait_send()
     for layer in range(2):
-        for j in range(CHUNKS):
+        for j in range(LINKS):
             for k in range(1, GROUP):
                 hand(layer, j, k).wait_send()
 
@@ -502,7 +560,7 @@
             def _():
                 hand(layer, j, 0).wait_send()
 
-    for j in range(CHUNKS):
+    for j in range(LINKS):
         for i in range(2):
             for k in range(GROUP):
                 at = j * 2 * GROUP + i * GROUP + k
@@ -530,7 +588,7 @@
     every = team * spt
     strip = reduced // STRIPS
     slab = reduced // n_s
-    cw = cols // CHUNKS
+    cw, zw = cols // CHUNKS, cols // LINKS
     kinds = 3 if n_s == 4 else n_s - 1
     f32, bf16 = jnp.float32, jnp.bfloat16
     vmem = pltpu.VMEM
@@ -543,6 +601,7 @@
         scratch_shapes=[
             vmem((GROUP, pool, reduced + tangents), f32),
             vmem((n_sec, reduced, cols), bf16),
+            vmem((reduced, cols), bf16),
             vmem(jacobian_targets.shape, bf16),
             vmem((every, reduced), f32),
             vmem((every, tangents), f32),
@@ -558,22 +617,23 @@
             vmem((STRIPS, QUADS - 1, high, strip), bf16),
             vmem((STRIPS, QUADS - 1, high, strip), bf16),
             vmem((STRIPS, team, high, strip), bf16),
-            vmem((CHUNKS, reduced, cw), f32),
-            vmem((CHUNKS, reduced, cw), bf16),
-            vmem((CHUNKS, kinds, slab, cw), bf16),
-            vmem((CHUNKS, slab, cw), bf16),
+            vmem((LINKS, reduced, zw), f32),
+            vmem((LINKS, reduced, zw), bf16),
+            vmem((LINKS, kinds, slab, zw), bf16),
+            vmem((LINKS, slab, zw), bf16),
             vmem((reduced, cols), f32),
             vmem((reduced, cols), bf16),
             vmem((kinds, slab, cols), bf16),
             vmem((slab, cols), bf16),
             vmem((every * tangents, cw), bf16),
             vmem((every, cw), f32),
-            vmem((n_sec, CHUNKS, GROUP, reduced // n_dp, cw), bf16),
-            dma(GROUP - 1), dma(GROUP - 1), dma(PIECES), dma(PIECES), dma(PIECES), dma(PIECES),
+            vmem((n_sec, LINKS, GROUP, reduced // n_dp, zw), bf16),
+            dma(GROUP - 1), dma(GROUP - 1), dma(PIECES + 1), dma(PIECES + 1),
+            dma(PIECES - 1), dma(PIECES - 1),
             dma(STRIPS), dma(STRIPS), dma(STRIPS * 3), dma(STRIPS * 3),
             dma(STRIPS * 3), dma(STRIPS * 3), dma(STRIPS * 4), dma(STRIPS * 4),
-            dma(kinds), dma(kinds), dma(CHUNKS * kinds), dma(CHUNKS * kinds),
-            dma(2 * CHUNKS * GROUP), dma(2 * CHUNKS * GROUP), dma(2),
+            dma(LASTS * kinds), dma(LASTS * kinds), dma(LINKS * kinds), dma(LINKS * kinds),
+            dma(2 * LINKS * GROUP), dma(2 * LINKS * GROUP), dma(3),
         ],
         compiler_params=pltpu.CompilerParams(
             collective_id=0, has_side_effects=True, vmem_limit_bytes=60 * 1024 * 1024

time: 94.6 us -> 89.6 us (0.947)
  Pallas kernels: 92.3 us -> 87.4 us
    pallas_call x1, Pallas kernels: 92.3 us -> 87.4 us  [shards(): pl.pallas_call(functools.partial(fused_kernel, n_s), out_shape=jax.ShapeD...]
where the time goes in v2:
time: 89.6 us; the launch traced here: 89.4 us
  Pallas kernels  87.4 us (98%)
  other arithmetic  2.08 us (2%)
    pallas_call x1, Pallas kernels, shards(): pl.pallas_call(functools.partial(fused_kernel, n_s), out_shape=jax.ShapeD...  87.4 us
    broadcast_in_dim x1, other arithmetic, shards(): return result.astype(f32)[None]  2.08 us

profile of v2, /device:TPU:0, one launch (start us, length us, event | category | flops | bytes accessed | tf_op | source)
XLA Modules:
  0.0 89.4 jit_solution(6701024537374005011)
XLA Ops:
  0.0 87.4 %fused.1 = bf16[32,8192]{1,0:T(8,128)(2,1)} custom-call(s32[1,8]{1,0:T(1,128)} %plan.1, bf16[8,512]{1,0:T(8,128)(2,1)} %samples.1, s32[8,128]{1,0:T(8,128)} %directions.1, bf16[8,512]{1,0:T(8,128)(2,1)} %targets.1, bf16[8,128,512]{2,1,0:T(8,128)(2,1)} %jac_hbm.1, bf16[1,512,8192]{2,1,0:T(8,128)(2,1)} %weight.1), custom_call_target="tpu_custom_call" | custom-call | tf_op jit(solution)/shard_map/fused/pallas_call | solution.py:596
  87.4 2.1 %bitcast_convert_fusion = f32[1,32,8192]{2,1,0:T(8,128)} fusion(bf16[32,8192]{1,0:T(8,128)(2,1)} %fused.1), kind=kLoop, calls=%fused_computation | loop fusion | flops 262144 | bytes 1572864 | tf_op jit(solution)/shard_map/broadcast_in_dim | solution.py:643

commit v3 on v2

--- a/solution.py
+++ b/solution.py
@@ -71,10 +71,10 @@
         return l * 2 + h, (base + h * 2 + core, l)
 
     if line:
-        opposite = lax.rem(s + 2, 4)
-        mate_opposite = lax.rem(mate + 2, 4)
-        others = [mate, opposite]
-        order = [mate_opposite, opposite, mate, s]
+        far_end, far_mid, across_z = 3 - 3 * (s // 2), 2 - s // 2, 3 - s
+        middle = lax.rem(s + 1, 4) >= 2
+        others = [mate]
+        order = [far_end, far_mid, mate, s]
         pairs = [1 - s // 2, s // 2]
     else:
         others = [lax.rem(s + k, n_s) for k in range(1, n_s)]
@@ -101,7 +101,16 @@
     ] + [(o * GROUP + g, sec) for o in others]
     for d, l in peers:
         pl.semaphore_signal(barrier, inc=1, device_id={"dp": d, "section": l})
-    pl.semaphore_wait(barrier, len(peers))
+    if line:
+
+        @pl.when(middle)
+        def _():
+            pl.semaphore_signal(
+                barrier, inc=1, device_id={"dp": across_z * GROUP + g, "section": sec}
+            )
+
+    pl.semaphore_wait(barrier, len(peers) + (jnp.where(middle, 1, 0) if line else 0))
+
 
     side = reduced // 2
     half_rows = pl.ds(pl.multiple_of(parity * side, side), side)
@@ -306,45 +315,62 @@
     def slab_of(o):
         return pl.ds(pl.multiple_of(o * slab, slab), slab)
 
-    def last_link(j, kind):
+    def last_link(j, kind, source=None, o=None):
         here = slice(j * lw, (j + 1) * lw)
-        if not line:
-            o = others[kind]
-            source = last_grads.at[slab_of(o), here]
-        elif kind == 2:
-            o, source = opposite, last_halves.at[:, here]
-        else:
-            o, source = mate, last_grads.at[slab_of([mate_opposite, mate][kind]), here]
+        if source is None:
+            o = others[kind] if not line else mate
+            slab_at = o if not line else order[min(kind, 2)]
+            source = last_grads.at[slab_of(slab_at), here]
         i = j * last_inbox.shape[0] + kind
         return remote(
             source, last_inbox.at[kind, :, here], s5.at[i], r5.at[i], o * GROUP + g, sec
         )
 
-    def last_relay(j):
-        last_link(j, 0).wait_recv()
-        here = slice(j * lw, (j + 1) * lw)
-        last_halves[:, here] = (
-            last_total[slab_of(opposite), here] + last_inbox[0, :, here].astype(f32)
-        ).astype(bf16)
-        last_link(j, 2).start()
-
-    def link(j, kind):
-        if not line:
-            o = others[kind]
-            source = grads.at[j, slab_of(o), :]
-        elif kind == 2:
-            o, source = opposite, halves.at[j]
-        else:
-            o, source = mate, grads.at[j, slab_of([mate_opposite, mate][kind]), :]
+    def link(j, kind, source=None, o=None):
+        if source is None:
+            o = others[kind] if not line else mate
+            slab_at = o if not line else order[min(kind, 2)]
+            source = grads.at[j, slab_of(slab_at), :]
         i = j * inbox.shape[1] + kind
         return remote(source, inbox.at[j, kind], s6.at[i], r6.at[i], o * GROUP + g, sec)
 
-    def relay(j):
-        link(j, 0).wait_recv()
-        halves[j] = (
-            total[j, slab_of(opposite), :] + inbox[j, 0].astype(f32)
-        ).astype(bf16)
-        link(j, 2).start()
+    if line:
+        turns = [(0, far_end, 3, across_z), (1, far_mid, 4, across_z), (3, mate, 2, mate)]
+
+    def last_onward(j, r):
+        return last_link(
+            j, turns[r][2], last_halves.at[r, :, slice(j * lw, (j + 1) * lw)], turns[r][3]
+        )
+
+    def last_relay(j, r):
+        @pl.when(middle)
+        def _():
+            kind, o, _, _ = turns[r]
+            here = slice(j * lw, (j + 1) * lw)
+            last_link(j, kind).wait_recv()
+            last_halves[r, :, here] = (
+                last_total[slab_of(o), here] + last_inbox[kind, :, here].astype(f32)
+            ).astype(bf16)
+            last_onward(j, r).start()
+
+    def onward(j, r):
+        return link(j, turns[r][2], halves.at[j, r], turns[r][3])
+
+    def relay(j, r):
+        @pl.when(middle)
+        def _():
+            kind, o, _, _ = turns[r]
+            link(j, kind).wait_recv()
+            halves[j, r] = (
+                total[j, slab_of(o), :] + inbox[j, kind].astype(f32)
+            ).astype(bf16)
+            onward(j, r).start()
+
+    def from_end(copies):
+        @pl.when(jnp.logical_not(middle))
+        def _():
+            for copy in copies:
+                copy.start()
 
     def columns(j):
         start = pl.multiple_of((sec * GROUP + g) * cols + j * zw, zw)
@@ -359,9 +385,7 @@
             base + h, layer,
         )
 
-    kinds = range(1, 3) if line else range(n_s - 1)
-
-    def finish(layer, j):
+    def add_up(layer, j, kinds):
         for h in range(GROUP):
             start = pl.multiple_of(s * slab + h * own_rows, own_rows)
             here = slice(h * own_rows, (h + 1) * own_rows)
@@ -375,6 +399,19 @@
                 for k in kinds:
                     value = value + inbox[j, k, here, :].astype(f32)
             finished[layer, j, h] = value.astype(bf16)
+
+    def finish(layer, j):
+        if line:
+
+            @pl.when(middle)
+            def _():
+                add_up(layer, j, (2, 4))
+
+            @pl.when(jnp.logical_not(middle))
+            def _():
+                add_up(layer, j, (2,))
+        else:
+            add_up(layer, j, range(n_s - 1))
         for k in range(1, GROUP):
             hand(layer, j, k).start()
 
@@ -386,9 +423,19 @@
         def _():
             columns(j)[...] = finished[layer, j, g]
 
+    def landed(j, one):
+        if line:
+            one(j, 2).wait_recv()
+
+            @pl.when(middle)
+            def _():
+                one(j, 4).wait_recv()
+        else:
+            for k in range(n_s - 1):
+                one(j, k).wait_recv()
+
     def arrived(j):
-        for k in kinds:
-            link(j, k).wait_recv()
+        landed(j, link)
 
     def backward(j):
         lo, hi = j * cw, (j + 1) * cw
@@ -467,55 +514,65 @@
     pass_on(order[0])
     last_of(order[0])
     if line:
-        for j in range(LASTS):
-            last_link(j, 0).start()
+        from_end([last_link(j, 0) for j in range(LASTS)])
     pass_on(order[1])
     last_of(order[1])
+    if line:
+        from_end([last_link(j, 1) for j in range(LASTS)])
     compare(order[2])
     if line:
-        last_relay(0)
+        last_relay(0, 0)
     compare(order[3])
     if line:
         for j in range(1, LASTS):
-            last_relay(j)
+            last_relay(j, 0)
     pass_on(order[2])
     last_of(order[2])
     if line:
-        for j in range(LASTS):
-            last_link(j, 1).start()
+        from_end([last_link(j, 2) for j in range(LASTS)])
     pass_on(order[3])
-    if line:
+    per_chunk = LINKS // CHUNKS
+    if line:
+        last_relay(0, 1)
         for k in range(QUADS):
             (passing(order[3], k) if k else gather(order[3], 0)).wait_recv()
-        turns = [
-            ([0, 1], [], []), ([2, 3], [], [0, 1]), ([4, 5], [0, 1], [2, 3]),
-            ([6, 7], [2, 3], [4, 5]),
-        ]
-        for j, (out_first, through, out_second) in enumerate(turns):
+        last_relay(0, 2)
+        for j in range(CHUNKS):
             backward(j)
-            for i in out_first:
-                link(i, 0).start()
-            for i in through:
-                relay(i)
-            for i in out_second:
-                link(i, 1).start()
+            pieces = range(j * per_chunk, (j + 1) * per_chunk)
+            from_end([link(i, k) for k in range(2) for i in pieces])
+            if j == 0:
+                for i in range(1, LASTS):
+                    last_relay(i, 1)
+                    last_relay(i, 2)
+            if j == 2:
+                for r in range(2):
+                    for i in range(2):
+                        relay(i, r)
+        from_end([link(i, 2) for i in range(LINKS)])
+        def pass_along(*pieces):
+            for r in range(2):
+                for i in pieces:
+                    relay(i, r)
+
+        def bring_back(*pieces):
+            for i in pieces:
+                relay(i, 2)
+
+        pass_along(2, 3)
+        bring_back(0, 1)
         own_strip()
-        relay(4)
-        relay(5)
-        link(6, 1).start()
-        link(7, 1).start()
+        pass_along(4, 5)
+        bring_back(2, 3)
         for i in range(LASTS):
-            for k in kinds:
-                last_link(i, k).wait_recv()
+            landed(i, last_link)
         for j in range(LINKS):
             finish(1, j)
-        arrived(0)
-        finish(0, 0)
-        arrived(1)
-        finish(0, 1)
-        relay(6)
-        relay(7)
-        for j in range(2, LINKS):
+        pass_along(6)
+        bring_back(4)
+        pass_along(7)
+        bring_back(5, 6, 7)
+        for j in range(LINKS):
             arrived(j)
             finish(0, j)
     else:
@@ -526,11 +583,10 @@
         for j in range(CHUNKS):
             backward(j)
             for kind in range(n_s - 1):
-                for i in range(j * LINKS // CHUNKS, (j + 1) * LINKS // CHUNKS):
+                for i in range(j * per_chunk, (j + 1) * per_chunk):
                     link(i, kind).start()
         for i in range(LASTS):
-            for k in kinds:
-                last_link(i, k).wait_recv()
+            landed(i, last_link)
         for j in range(LINKS):
             finish(1, j)
         for j in range(LINKS):
@@ -546,11 +602,29 @@
             passing(p, k).wait_send()
         for k in range(QUADS):
             gather(p, k).wait_send()
-    for k in range(last_inbox.shape[0]):
-        for j in range(LASTS):
-            last_link(j, k).wait_send()
-        for j in range(LINKS):
-            link(j, k).wait_send()
+    if line:
+
+        @pl.when(middle)
+        def _():
+            for r in range(3):
+                for j in range(LASTS):
+                    last_onward(j, r).wait_send()
+                for j in range(LINKS):
+                    onward(j, r).wait_send()
+
+        @pl.when(jnp.logical_not(middle))
+        def _():
+            for k in range(3):
+                for j in range(LASTS):
+                    last_link(j, k).wait_send()
+                for j in range(LINKS):
+                    link(j, k).wait_send()
+    else:
+        for k in range(n_s - 1):
+            for j in range(LASTS):
+                last_link(j, k).wait_send()
+            for j in range(LINKS):
+                link(j, k).wait_send()
     for layer in range(2):
         for j in range(LINKS):
             for k in range(1, GROUP):
@@ -589,7 +663,7 @@
     strip = reduced // STRIPS
     slab = reduced // n_s
     cw, zw = cols // CHUNKS, cols // LINKS
-    kinds = 3 if n_s == 4 else n_s - 1
+    kinds = 5 if n_s == 4 else n_s - 1
     f32, bf16 = jnp.float32, jnp.bfloat16
     vmem = pltpu.VMEM
     dma = lambda n: pltpu.SemaphoreType.DMA((n,))
@@ -620,11 +694,11 @@
             vmem((LINKS, reduced, zw), f32),
             vmem((LINKS, reduced, zw), bf16),
             vmem((LINKS, kinds, slab, zw), bf16),
-            vmem((LINKS, slab, zw), bf16),
+            vmem((LINKS, 3, slab, zw), bf16),
             vmem((reduced, cols), f32),
             vmem((reduced, cols), bf16),
             vmem((kinds, slab, cols), bf16),
-            vmem((slab, cols), bf16),
+            vmem((3, slab, cols), bf16),
             vmem((every * tangents, cw), bf16),
             vmem((every, cw), f32),
             vmem((n_sec, LINKS, GROUP, reduced // n_dp, zw), bf16),

time: 89.6 us -> 86.2 us (0.962)
  Pallas kernels: 87.4 us -> 83.9 us
    pallas_call x1, Pallas kernels: 87.4 us -> 83.9 us  [shards(): pl.pallas_call(functools.partial(fused_kernel, n_s), out_shape=jax.ShapeD...]
where the time goes in v3:
time: 86.2 us; the launch traced here: 86 us
  Pallas kernels  83.9 us (97%)
  other arithmetic  2.08 us (2%)
    pallas_call x1, Pallas kernels, shards(): pl.pallas_call(functools.partial(fused_kernel, n_s), out_shape=jax.ShapeD...  83.9 us
    broadcast_in_dim x1, other arithmetic, shards(): return result.astype(f32)[None]  2.08 us

profile of v3, /device:TPU:0, one launch (start us, length us, event | category | flops | bytes accessed | tf_op | source)
XLA Modules:
  0.0 86.0 jit_solution(10013679927102812179)
XLA Ops:
  0.0 83.9 %fused.1 = bf16[32,8192]{1,0:T(8,128)(2,1)} custom-call(s32[1,8]{1,0:T(1,128)} %plan.1, bf16[8,512]{1,0:T(8,128)(2,1)} %samples.1, s32[8,128]{1,0:T(8,128)} %directions.1, bf16[8,512]{1,0:T(8,128)(2,1)} %targets.1, bf16[8,128,512]{2,1,0:T(8,128)(2,1)} %jac_hbm.1, bf16[1,512,8192]{2,1,0:T(8,128)(2,1)} %weight.1), custom_call_target="tpu_custom_call" | custom-call | tf_op jit(solution)/shard_map/fused/pallas_call | solution.py:670
  83.9 2.1 %bitcast_convert_fusion = f32[1,32,8192]{2,1,0:T(8,128)} fusion(bf16[32,8192]{1,0:T(8,128)(2,1)} %fused.1), kind=kLoop, calls=%fused_computation | loop fusion | flops 262144 | bytes 1572864 | tf_op jit(solution)/shard_map/broadcast_in_dim | solution.py:717

commit v4 on v3

--- a/solution.py
+++ b/solution.py
@@ -19,7 +19,6 @@
 
 jacobian_weight = 32.0
 
-VMEM = pl.BlockSpec(memory_space=pltpu.VMEM)
 ANY = pl.BlockSpec(memory_space=pl.ANY)
 
 
@@ -31,8 +30,8 @@
 
 
 def fused_kernel(
-    n_s, plan, samples, directions, targets, jac_hbm, weight, out,
-    packs, both, mail, jac, xs, dirs, onehot_t, onehot, act, hidden, picked, first, second,
+    n_s, plan, samples_hbm, directions_hbm, targets_hbm, jac_hbm, weight, out,
+    samples, directions, targets, packs, both, mail, jac, xs, dirs, onehot_t, onehot, act, hidden, picked, first, second,
     partial, first_in, sums, second_in, misfit, total, grads, inbox, halves,
     last_total, last_grads, last_inbox, last_halves, pulled, proj, finished,
     psend, precv, wsend, wrecv, zsend, zrecv, s1, r1, s2, r2, s3, r3, s4, r4,
@@ -93,6 +92,14 @@
     own.start()
     load_jac = pltpu.make_async_copy(jac_hbm, jac, local.at[1])
     load_jac.start()
+    loads = [
+        pltpu.make_async_copy(a, b, local.at[4 + i])
+        for i, (a, b) in enumerate(
+            ((samples_hbm, samples), (directions_hbm, directions), (targets_hbm, targets))
+        )
+    ]
+    for copy in loads:
+        copy.start()
 
     barrier = pltpu.get_barrier_semaphore()
     peers = [
@@ -120,10 +127,12 @@
     for c in range(PIECES + 1):
         here = (half_rows if c < PIECES else other_rows, pl.ds(min(c, PIECES - 1) * pw, pw))
         sent.append(remote(
-            mail.at[here], both.at[(sec,) + here], wsend.at[c], wrecv.at[c], dp, 1 - sec,
+            mail.at[here], both.at[(sec,) + here], wsend, wrecv.at[c], dp, 1 - sec,
         ))
         sent[-1].start()
 
+    for copy in loads:
+        copy.wait()
     every = jnp.concatenate(
         [samples[...].astype(f32), directions[...].astype(f32)], axis=1
     )
@@ -136,7 +145,7 @@
     shared = []
     for k in range(1, GROUP):
         shared.append(remote(
-            packs.at[g], packs.at[g], psend.at[k - 1], precv.at[k - 1],
+            packs.at[g], packs.at[g], psend, precv,
             base + lax.rem(g + k, GROUP), sec,
         ))
         shared[-1].start()
@@ -145,12 +154,12 @@
         sent[c].wait_recv()
         if c < PIECES - 1:
             came = both.at[1 - sec, half_rows, pl.ds(c * pw, pw)]
-            relayed.append(remote(came, came, zsend.at[c], zrecv.at[c], *twin))
+            relayed.append(remote(came, came, zsend, zrecv.at[c], *twin))
             relayed[-1].start()
 
     arrive(0)
-    for copy in shared:
-        copy.wait_recv()
+    several = packs.at[0 : GROUP - 1]
+    remote(several, several, psend, precv, *partner).wait_recv()
     for b in range(2 * QUADS):
         c, l, h = b // QUADS, (b % QUADS) // 2, b % 2
         xs[b * spt : (b + 1) * spt] = packs[h * 2 + c, l * spt : (l + 1) * spt, :reduced]
@@ -230,28 +239,28 @@
     def across(p):
         theirs = pl.ds(pl.multiple_of((1 - core) * QUADS, QUADS), QUADS)
         return remote(
-            partial.at[p, theirs], first_in.at[p], s1.at[p], r1.at[p], *partner
+            partial.at[p, theirs], first_in.at[p], s1, r1.at[p], *partner
         )
 
     def away(p, k):
         return remote(
             sums.at[p, k - 1], second_in.at[p, k - 1],
-            s2.at[p * 3 + k - 1], r2.at[p * 3 + k - 1], *quad(k)[1],
+            s2, r2.at[p], *quad(k)[1],
         )
 
     def gather(p, k):
         if k == 0:
             return remote(
-                misfit.at[p, mine], misfit.at[p, mine], s4.at[p * 4], r4.at[p * 4], *partner
+                misfit.at[p, mine], misfit.at[p, mine], s4, r4.at[p], *partner
             )
         return remote(
             misfit.at[p, mine], misfit.at[p, mine],
-            s3.at[p * 3 + k - 1], r3.at[p * 3 + k - 1], *quad(k)[1],
+            s3, r3.at[p * 3 + k - 1], *quad(k)[1],
         )
 
     def passing(p, k):
         came = misfit.at[p, core * QUADS + quad(k)[0]]
-        return remote(came, came, s4.at[p * 4 + k], r4.at[p * 4 + k], *partner)
+        return remote(came, came, s4, r4.at[p], *partner)
 
     def reduce_out(p):
         across(p).wait_recv()
@@ -263,8 +272,7 @@
             away(p, k).start()
 
     def compare(p):
-        for k in range(1, QUADS):
-            away(p, k).wait_recv()
+        remote(sums.at[p], second_in.at[p], s2, r2.at[p], *partner).wait_recv()
         lanes = pl.ds(pl.multiple_of(p * strip, strip), strip)
 
         def whole(lo, hi):
@@ -297,9 +305,12 @@
             gather(p, k).wait_recv()
             passing(p, k).start()
 
+    def others_in(p):
+        theirs = misfit.at[p, pl.ds(pl.multiple_of((1 - core) * QUADS, QUADS), QUADS)]
+        remote(theirs, theirs, s4, r4.at[p], *partner).wait_recv()
+
     def last_of(p):
-        for k in range(QUADS):
-            (passing(p, k) if k else gather(p, 0)).wait_recv()
+        others_in(p)
         lhs = jnp.concatenate([misfit[p, b, 0:rows] for b in range(2 * QUADS)], axis=0)
         value = lax.dot_general(lhs, act[...], over_rows, preferred_element_type=f32)
         tail = misfit[p, 0, rows:].astype(f32)
@@ -323,7 +334,7 @@
             source = last_grads.at[slab_of(slab_at), here]
         i = j * last_inbox.shape[0] + kind
         return remote(
-            source, last_inbox.at[kind, :, here], s5.at[i], r5.at[i], o * GROUP + g, sec
+            source, last_inbox.at[kind, :, here], s5, r5.at[i], o * GROUP + g, sec
         )
 
     def link(j, kind, source=None, o=None):
@@ -332,7 +343,7 @@
             slab_at = o if not line else order[min(kind, 2)]
             source = grads.at[j, slab_of(slab_at), :]
         i = j * inbox.shape[1] + kind
-        return remote(source, inbox.at[j, kind], s6.at[i], r6.at[i], o * GROUP + g, sec)
+        return remote(source, inbox.at[j, kind], s6, r6.at[i], o * GROUP + g, sec)
 
     if line:
         turns = [(0, far_end, 3, across_z), (1, far_mid, 4, across_z), (3, mate, 2, mate)]
@@ -376,14 +387,12 @@
         start = pl.multiple_of((sec * GROUP + g) * cols + j * zw, zw)
         return out.at[:, pl.ds(start, zw)]
 
+    def keep(j):
+        return pltpu.make_async_copy(finished.at[sec, j, g], columns(j), local.at[3])
+
     def hand(layer, j, k):
         h = lax.rem(g + k, GROUP)
-        i = j * 2 * GROUP
-        return remote(
-            finished.at[layer, j, h], columns(j),
-            s7.at[layer * LINKS * GROUP + j * GROUP + k], r7.at[i + sec * GROUP + k],
-            base + h, layer,
-        )
+        return remote(finished.at[layer, j, h], columns(j), s7, r7, base + h, layer)
 
     def add_up(layer, j, kinds):
         for h in range(GROUP):
@@ -421,7 +430,7 @@
 
         @pl.when(sec == layer)
         def _():
-            columns(j)[...] = finished[layer, j, g]
+            keep(j).start()
 
     def landed(j, one):
         if line:
@@ -534,8 +543,7 @@
     per_chunk = LINKS // CHUNKS
     if line:
         last_relay(0, 1)
-        for k in range(QUADS):
-            (passing(order[3], k) if k else gather(order[3], 0)).wait_recv()
+        others_in(order[3])
         last_relay(0, 2)
         for j in range(CHUNKS):
             backward(j)
@@ -563,15 +571,17 @@
         bring_back(0, 1)
         own_strip()
         pass_along(4, 5)
-        bring_back(2, 3)
+        bring_back(2)
         for i in range(LASTS):
             landed(i, last_link)
         for j in range(LINKS):
             finish(1, j)
-        pass_along(6)
-        bring_back(4)
-        pass_along(7)
-        bring_back(5, 6, 7)
+        relay(6, 0)
+        relay(7, 0)
+        bring_back(3)
+        relay(6, 1)
+        relay(7, 1)
+        bring_back(4, 5, 6, 7)
         for j in range(LINKS):
             arrived(j)
             finish(0, j)
@@ -593,61 +603,23 @@
             arrived(j)
             finish(0, j)
 
-    for copy in shared + sent + relayed:
-        copy.wait_send()
-    for p in range(STRIPS):
-        across(p).wait_send()
-        for k in range(1, QUADS):
-            away(p, k).wait_send()
-            passing(p, k).wait_send()
-        for k in range(QUADS):
-            gather(p, k).wait_send()
-    if line:
-
-        @pl.when(middle)
-        def _():
-            for r in range(3):
-                for j in range(LASTS):
-                    last_onward(j, r).wait_send()
-                for j in range(LINKS):
-                    onward(j, r).wait_send()
-
-        @pl.when(jnp.logical_not(middle))
-        def _():
-            for k in range(3):
-                for j in range(LASTS):
-                    last_link(j, k).wait_send()
-                for j in range(LINKS):
-                    link(j, k).wait_send()
-    else:
-        for k in range(n_s - 1):
-            for j in range(LASTS):
-                last_link(j, k).wait_send()
-            for j in range(LINKS):
-                link(j, k).wait_send()
-    for layer in range(2):
-        for j in range(LINKS):
-            for k in range(1, GROUP):
-                hand(layer, j, k).wait_send()
-
-            @pl.when(sec != layer)
-            def _():
-                hand(layer, j, 0).wait_send()
-
-    for j in range(LINKS):
-        for i in range(2):
-            for k in range(GROUP):
-                at = j * 2 * GROUP + i * GROUP + k
-                arrival = remote(
-                    finished.at[0, j, 0], columns(j), s7.at[0], r7.at[at], *partner
-                )
-                if k:
-                    arrival.wait_recv()
-                else:
-
-                    @pl.when(sec != i)
-                    def _():
-                        arrival.wait_recv()
+    def all_sent(ref, send):
+        remote(ref, ref, send, precv, *partner).wait_send()
+
+    all_sent(packs.at[0 : GROUP - 1], psend)
+    all_sent(mail.at[0 : (PIECES + 1) * side * pw // cols], wsend)
+    all_sent(mail.at[0 : (PIECES - 1) * side * pw // cols], zsend)
+    all_sent(first_in, s1)
+    all_sent(second_in, s2)
+    all_sent(second_in, s3)
+    all_sent(first_in, s4)
+    all_sent(last_halves if line else last_inbox, s5)
+    all_sent(halves if line else inbox, s6)
+    rest = out.at[:, 0 : (2 * GROUP - 1) * cols]
+    all_sent(rest, s7)
+    own_kept = finished.at[0, :, 0]
+    pltpu.make_async_copy(own_kept, own_kept, local.at[3]).wait()
+    remote(rest, rest, s7, r7, *partner).wait_recv()
 
 
 def shards(n_dp, n_sec, samples, targets, jacobian_targets, directions, plan, weights):
@@ -667,12 +639,16 @@
     f32, bf16 = jnp.float32, jnp.bfloat16
     vmem = pltpu.VMEM
     dma = lambda n: pltpu.SemaphoreType.DMA((n,))
+    one = pltpu.SemaphoreType.DMA
     result = pl.pallas_call(
         functools.partial(fused_kernel, n_s),
         out_shape=jax.ShapeDtypeStruct((reduced // n_dp, width), bf16),
-        in_specs=[pl.BlockSpec(memory_space=pltpu.SMEM), VMEM, VMEM, VMEM, ANY, ANY],
-        out_specs=VMEM,
+        in_specs=[pl.BlockSpec(memory_space=pltpu.SMEM)] + [ANY] * 5,
+        out_specs=ANY,
         scratch_shapes=[
+            vmem(samples.shape, bf16),
+            vmem(directions.shape, jnp.int32),
+            vmem(targets.shape, bf16),
             vmem((GROUP, pool, reduced + tangents), f32),
             vmem((n_sec, reduced, cols), bf16),
             vmem((reduced, cols), bf16),
@@ -702,12 +678,9 @@
             vmem((every * tangents, cw), bf16),
             vmem((every, cw), f32),
             vmem((n_sec, LINKS, GROUP, reduced // n_dp, zw), bf16),
-            dma(GROUP - 1), dma(GROUP - 1), dma(PIECES + 1), dma(PIECES + 1),
-            dma(PIECES - 1), dma(PIECES - 1),
-            dma(STRIPS), dma(STRIPS), dma(STRIPS * 3), dma(STRIPS * 3),
-            dma(STRIPS * 3), dma(STRIPS * 3), dma(STRIPS * 4), dma(STRIPS * 4),
-            dma(LASTS * kinds), dma(LASTS * kinds), dma(LINKS * kinds), dma(LINKS * kinds),
-            dma(2 * LINKS * GROUP), dma(2 * LINKS * GROUP), dma(3),
+            one, one, one, dma(PIECES + 1), one, dma(PIECES - 1),
+            one, dma(STRIPS), one, dma(STRIPS), one, dma(STRIPS * 3), one, dma(STRIPS),
+            one, dma(LASTS * kinds), one, dma(LINKS * kinds), one, one, dma(7),
         ],
         compiler_params=pltpu.CompilerParams(
             collective_id=0, has_side_effects=True, vmem_limit_bytes=60 * 1024 * 1024

time: 86.2 us -> 82.5 us (0.957)
  Pallas kernels: 83.9 us -> 80.2 us
    pallas_call x1, Pallas kernels: 83.9 us -> 80.2 us  [shards(): pl.pallas_call(functools.partial(fused_kernel, n_s), out_shape=jax.ShapeD...]
where the time goes in v4:
time: 82.5 us; the launch traced here: 82.3 us
  Pallas kernels  80.2 us (97%)
  other arithmetic  2.08 us (3%)
    pallas_call x1, Pallas kernels, shards(): pl.pallas_call(functools.partial(fused_kernel, n_s), out_shape=jax.ShapeD...  80.2 us
    broadcast_in_dim x1, other arithmetic, shards(): return result.astype(f32)[None]  2.08 us

profile of v4, /device:TPU:0, one launch (start us, length us, event | category | flops | bytes accessed | tf_op | source)
XLA Modules:
  0.0 82.3 jit_solution(16445663867228124033)
XLA Ops:
  0.0 80.2 %fused.1 = bf16[32,8192]{1,0:T(8,128)(2,1)} custom-call(s32[1,8]{1,0:T(1,128)} %plan.1, bf16[8,512]{1,0:T(8,128)(2,1)} %samples_hbm.1, s32[8,128]{1,0:T(8,128)} %directions_hbm.1, bf16[8,512]{1,0:T(8,128)(2,1)} %targets_hbm.1, bf16[8,128,512]{2,1,0:T(8,128)(2,1)} %jac_hbm.1, bf16[1,512,8192]{2,1,0:T(8,128)(2,1)} %weight.1), custom_call_target="tpu_custom_call" | custom-call | tf_op jit(solution)/shard_map/fused/pallas_call | solution.py:643
  80.3 2.1 %bitcast_convert_fusion = f32[1,32,8192]{2,1,0:T(8,128)} fusion(bf16[32,8192]{1,0:T(8,128)(2,1)} %fused.1), kind=kLoop, calls=%fused_computation | loop fusion | flops 262144 | bytes 1572864 | tf_op jit(solution)/shard_map/broadcast_in_dim | solution.py:690

commit v5 on v4

--- a/solution.py
+++ b/solution.py
@@ -545,43 +545,42 @@
         last_relay(0, 1)
         others_in(order[3])
         last_relay(0, 2)
+        def pass_along(r, *pieces):
+            for i in pieces:
+                relay(i, r)
+
         for j in range(CHUNKS):
             backward(j)
-            pieces = range(j * per_chunk, (j + 1) * per_chunk)
-            from_end([link(i, k) for k in range(2) for i in pieces])
+            pieces = list(range(j * per_chunk, (j + 1) * per_chunk))
+            before = [i - per_chunk for i in pieces if j]
+            rest_too = j == CHUNKS - 1
+            from_end(
+                [link(i, 0) for i in pieces]
+                + [link(i, 1) for i in before + (pieces if rest_too else [])]
+                + [link(i, 2) for i in range(LINKS if rest_too else 0)]
+            )
             if j == 0:
                 for i in range(1, LASTS):
                     last_relay(i, 1)
                     last_relay(i, 2)
             if j == 2:
-                for r in range(2):
-                    for i in range(2):
-                        relay(i, r)
-        from_end([link(i, 2) for i in range(LINKS)])
-        def pass_along(*pieces):
-            for r in range(2):
-                for i in pieces:
-                    relay(i, r)
-
-        def bring_back(*pieces):
-            for i in pieces:
-                relay(i, 2)
-
-        pass_along(2, 3)
-        bring_back(0, 1)
+                pass_along(0, 0, 1)
+        pass_along(0, 2, 3)
+        pass_along(1, 0, 1)
+        pass_along(0, 4, 5)
+        pass_along(2, 0, 1)
         own_strip()
-        pass_along(4, 5)
-        bring_back(2)
+        pass_along(1, 2, 3)
+        pass_along(0, 6, 7)
+        pass_along(2, 2, 3)
         for i in range(LASTS):
             landed(i, last_link)
         for j in range(LINKS):
             finish(1, j)
-        relay(6, 0)
-        relay(7, 0)
-        bring_back(3)
-        relay(6, 1)
-        relay(7, 1)
-        bring_back(4, 5, 6, 7)
+        pass_along(1, 4, 5)
+        pass_along(2, 4, 5)
+        pass_along(1, 6, 7)
+        pass_along(2, 6, 7)
         for j in range(LINKS):
             arrived(j)
             finish(0, j)

time: 82.5 us -> 81.1 us (0.983)
  Pallas kernels: 80.2 us -> 78.8 us
    pallas_call x1, Pallas kernels: 80.2 us -> 78.8 us  [shards(): pl.pallas_call(functools.partial(fused_kernel, n_s), out_shape=jax.ShapeD...]
where the time goes in v5:
time: 81.1 us; the launch traced here: 80.9 us
  Pallas kernels  78.8 us (97%)
  other arithmetic  2.08 us (3%)
    pallas_call x1, Pallas kernels, shards(): pl.pallas_call(functools.partial(fused_kernel, n_s), out_shape=jax.ShapeD...  78.8 us
    broadcast_in_dim x1, other arithmetic, shards(): return result.astype(f32)[None]  2.08 us

profile of v5, /device:TPU:0, one launch (start us, length us, event | category | flops | bytes accessed | tf_op | source)
XLA Modules:
  0.0 80.9 jit_solution(661322445529137562)
XLA Ops:
  0.0 78.8 %fused.1 = bf16[32,8192]{1,0:T(8,128)(2,1)} custom-call(s32[1,8]{1,0:T(1,128)} %plan.1, bf16[8,512]{1,0:T(8,128)(2,1)} %samples_hbm.1, s32[8,128]{1,0:T(8,128)} %directions_hbm.1, bf16[8,512]{1,0:T(8,128)(2,1)} %targets_hbm.1, bf16[8,128,512]{2,1,0:T(8,128)(2,1)} %jac_hbm.1, bf16[1,512,8192]{2,1,0:T(8,128)(2,1)} %weight.1), custom_call_target="tpu_custom_call" | custom-call | tf_op jit(solution)/shard_map/fused/pallas_call | solution.py:642
  78.8 2.1 %bitcast_convert_fusion = f32[1,32,8192]{2,1,0:T(8,128)} fusion(bf16[32,8192]{1,0:T(8,128)(2,1)} %fused.1), kind=kLoop, calls=%fused_computation | loop fusion | flops 262144 | bytes 1572864 | tf_op jit(solution)/shard_map/broadcast_in_dim | solution.py:689
